TPU v7x, 1024 devices: a whole 8x8x8 slice. The times are simulated.
1024 devices in a mesh: mem: 32 (over y_hi, x), strip: 32 (over z, y_lo, core).
Axes of the slice: x: 8, y: 8 (y_hi: 4, y_lo: 2; y = y_hi * 2 + y_lo), z: 8, core: 2. Of those that a mesh axis runs over, the one named last changes fastest.
Arguments:
- ensemble: float32 [256, 256, 2048], P('mem', 'strip'), may hold values from -12 to 12
- forcing: float32 [256, 2048], P('strip'), may hold values from 4 to 12
- obs_index: int32 [2048, 128], P(('strip', 'mem')), may hold values from 0 to 255
- obs_count: int32 [2048], P(('strip', 'mem')), may hold values from 1 to 128, as said below
- obs_value: float32 [2048, 128], P(('strip', 'mem')), may hold values from -18 to 18
- obs_precision: float32 [2048, 128], P(('strip', 'mem')), may hold values from 0.05 to 1
Outputs:
- analysis: float32 [256, 256, 2048], P('mem', 'strip')
Inputs may be any that keep to these rules, and one draw needn't show every extreme that they name: The live observations of a region are the first obs_count of its slots; in every draw some region has all 128 slots live. `obs_index`: position of the observed cell within its region; a cell may be observed more than once.
All inputs are finite; a program needn't handle non-finite values.
Results may differ from a plain program's by a relative error of at most 0.0003.
Values sent between devices are 32-bit elements; how exact they have to be, the bound alone decides.
No kernel may reach another device: no remote copies, remote signals or barrier semaphores. Data moves between devices by JAX's collectives and lax.ppermute only.
A program may use at most 32 MiB of HBM per device.

v0:
```python
import math

import jax
import jax.numpy as jnp
from jax import lax
from jax.sharding import PartitionSpec as P

STEPS = 4
NS_ITERS = 4
REGION_VALUES = 256


step_size = 0.05
coupling = 0.4


def padded(block, sides, width):
    for axis, dim in sides:
        count = lax.axis_size(axis)
        forward = [(i, i + 1) for i in range(count - 1)]
        backward = [(target, source) for source, target in forward]
        low = lax.ppermute(
            lax.slice_in_dim(block, block.shape[dim] - width, None, axis=dim), axis, forward
        )
        high = lax.ppermute(lax.slice_in_dim(block, 0, width, axis=dim), axis, backward)
        block = jnp.concatenate([low, block, high], axis=dim)
    return block


def march_forward(padded_state, forcing_rows):
    center = padded_state[:, 1:-1]
    meridional = padded_state[:, 2:] + padded_state[:, :-2] - 2.0 * center
    advection = (jnp.roll(center, -1, 2) - jnp.roll(center, 2, 2)) * jnp.roll(center, 1, 2)
    return center + step_size * (advection - center + forcing_rows) + coupling * meridional


def analyze(members, obs_index, obs_count, obs_value, obs_precision):
    highest = lax.Precision.HIGHEST
    ens_size = members.shape[0]
    member_mean = jnp.mean(members, axis=0)
    spread = members - member_mean[None]
    cell_ids = jnp.arange(members.shape[2], dtype=jnp.int32)
    onehot = (obs_index[:, :, None] == cell_ids[None, None, :]).astype(jnp.float32)
    slot_ids = jnp.arange(obs_index.shape[1], dtype=jnp.int32)
    live_mask = (slot_ids[None, :] < obs_count[:, None]).astype(jnp.float32)
    obs_spread = jnp.einsum("roc,krc->rok", onehot, spread, precision=highest)
    obs_mean = jnp.einsum("roc,rc->ro", onehot, member_mean, precision=highest)
    weight = obs_precision * live_mask
    innovation = weight * (obs_value - obs_mean)
    gram_matrix = jnp.einsum(
        "roj,rok->rjk", obs_spread * weight[:, :, None], obs_spread, precision=highest
    )
    identity = jnp.eye(ens_size, dtype=jnp.float32)
    norm_scale = ens_size - 1.0 + jnp.sqrt(jnp.sum(gram_matrix * gram_matrix, axis=(1, 2)))
    left_iterate = ((ens_size - 1.0) * identity + gram_matrix) / norm_scale[:, None, None]
    right_iterate = jnp.broadcast_to(identity, gram_matrix.shape)
    for repeat in range(NS_ITERS):
        correction = 1.5 * identity - 0.5 * jnp.einsum(
            "rij,rjk->rik", right_iterate, left_iterate, precision=highest
        )
        left_iterate = jnp.einsum("rij,rjk->rik", left_iterate, correction, precision=highest)
        right_iterate = jnp.einsum("rij,rjk->rik", correction, right_iterate, precision=highest)
    inv_root = right_iterate / jnp.sqrt(norm_scale)[:, None, None]
    projected = jnp.einsum("roj,ro->rj", obs_spread, innovation, precision=highest)
    halfway = jnp.einsum("rjk,rk->rj", inv_root, projected, precision=highest)
    mean_weights = jnp.einsum("rjk,rk->rj", inv_root, halfway, precision=highest)
    transform = math.sqrt(ens_size - 1.0) * inv_root + mean_weights[:, :, None]
    return member_mean[None] + jnp.einsum("rjk,jrc->krc", transform, spread, precision=highest)


def local(ensemble, forcing, obs_index, obs_count, obs_value, obs_precision):
    regional_members, latitude_rows, longitude_cells = ensemble.shape
    stacked = jnp.concatenate([ensemble, forcing[None]], axis=0)
    padded_state = padded(stacked, (("strip", 1),), STEPS)
    forcing_pad = padded_state[regional_members]
    current = padded_state[:regional_members]
    strip_id = lax.axis_index("strip")
    global_rows = strip_id * latitude_rows + jnp.arange(
        -STEPS, latitude_rows + STEPS, dtype=jnp.int32
    )
    inside = ((global_rows >= 0) & (global_rows < latitude_rows * lax.axis_size("strip"))).astype(
        jnp.float32
    )
    for sweep_index in range(STEPS):
        rows_next = current.shape[1] - 2
        advanced = march_forward(
            current, forcing_pad[sweep_index + 1 : sweep_index + 1 + rows_next]
        )
        current = advanced * inside[sweep_index + 1 : sweep_index + 1 + rows_next][None, :, None]
    flat_state = current.reshape(regional_members, latitude_rows * longitude_cells)
    mem_count = lax.axis_size("mem")
    region_cells = latitude_rows * longitude_cells // mem_count
    regional = lax.all_to_all(flat_state, "mem", split_axis=1, concat_axis=0, tiled=True)
    blocks = regional.reshape(regional.shape[0], region_cells // REGION_VALUES, REGION_VALUES)
    analysis = analyze(blocks, obs_index, obs_count, obs_value, obs_precision)
    analysis = analysis.reshape(regional.shape[0], region_cells)
    members_back = lax.all_to_all(analysis, "mem", split_axis=0, concat_axis=1, tiled=True)
    return members_back.reshape(regional_members, latitude_rows, longitude_cells)


def solution(mesh):
    placed = (
        P("mem", "strip", None),
        P("strip", None),
        P(("strip", "mem"), None),
        P(("strip", "mem")),
        P(("strip", "mem"), None),
        P(("strip", "mem"), None),
    )
    return jax.shard_map(
        local, mesh=mesh, in_specs=placed, out_specs=P("mem", "strip", None), check_vma=False
    )
```

profile of v0, /device:TPU:258, one launch (start us, length us, event | category | flops | bytes accessed | tf_op | source)
XLA Modules:
  0.0 99.3 jit_solution(6920015733678796740)
XLA Ops:
  0.0 1.5 %fusion.49 = (f32[9,4,2048]{2,1,0:T(4,128)S(1)}, f32[9,4,2048]{2,1,0:T(4,128)S(1)}) fusion(f32[8,8,2048]{2,1,0:T(8,128)} %param.6, f32[1,8,2048]{2,1,0:T(8,128)} %bitcast.61), kind=kLoop, calls=%fused_computation.76 | loop fusion | flops 147456 | bytes 1179648 | tf_op jit(solution)/shard_map/concatenate | solution.py:73
  1.5 0.2 copy.28
  1.7 1.9 %collective-permute-start = (f32[9,4,2048]{2,0,1:T(8,128)S(1)}, f32[9,4,2048]{2,0,1:T(8,128)S(1)}, u32[]{:S(2)}, u32[]{:S(2)}) collective-permute-start(f32[9,4,2048]{2,0,1:T(8,128)S(1)} %copy.28), channel_id=1, source_target_pairs={{0,1},{1,2},{2,3},{3,4},{4,5},{5,6},{6,7},{7,8},{8,9},{9,10},{10,1... | collective-permute-start | bytes 884744 | tf_op jit(solution)/shard_map/ppermute | solution.py:22
  3.6 0.2 copy.29
  3.8 4.5 %collective-permute-start.1 = (f32[9,4,2048]{2,0,1:T(8,128)S(1)}, f32[9,4,2048]{2,0,1:T(8,128)S(1)}, u32[]{:S(2)}, u32[]{:S(2)}) collective-permute-start(f32[9,4,2048]{2,0,1:T(8,128)S(1)} %copy.29), channel_id=1, source_target_pairs={{1,0},{2,1},{3,2},{4,3},{5,4},{6,5},{7,6},{8,7},{9,8},{10,9},{11,1... | collective-permute-start | bytes 884744 | tf_op jit(solution)/shard_map/ppermute | solution.py:25
  8.4 0.1 slice.210
  8.5 0.1 slice.221
  8.5 0.1 slice.232
  8.6 0.1 slice.242
  8.7 8.6 %collective-permute-done = f32[9,4,2048]{2,0,1:T(8,128)S(1)} collective-permute-done((f32[9,4,2048]{2,0,1:T(8,128)S(1)}, f32[9,4,2048]{2,0,1:T(8,128)S(1)}, u32[]{:S(2)}, u32[]{:S(2)}) %collective-permute-start) | collective-permute-done | bytes 294944 | tf_op jit(solution)/shard_map/ppermute | solution.py:22
  17.3 0.2 copy.30
  17.5 0.2 copy.31
  17.7 0.2 pad_maximum_fusion
  17.9 0.4 fusion.70
  18.3 0.1 slice.247
  18.5 0.9 fusion.16
  19.3 0.4 fusion.76
  19.7 0.1 fusion.75
  19.8 0.1 slice.256
  20.0 0.1 slice.255
  20.1 0.8 fusion.12
  20.9 0.4 fusion.74
  21.3 0.1 slice.266
  21.4 0.1 fusion.73
  21.5 0.1 slice.265
  21.6 0.8 fusion.8
  22.5 0.2 fusion.72
  22.7 0.1 slice.276
  22.7 0.1 fusion.71
  22.8 0.1 slice.275
  22.9 0.4 fusion.39
  23.3 0.1 all_to_all.24
  23.5 1.1 %copy.32 = f32[8,32,512]{2,0,1:T(8,128)} copy(f32[8,32,512]{2,1,0:T(8,128)S(1)} %all_to_all.24) | data formatting | bytes 1048576 | tf_op jit(solution)/shard_map/all_to_all | solution.py:93
  24.6 14.1 %all-to-all-start = ((f32[8,32,512]{2,0,1:T(8,128)}), f32[8,32,512]{2,0,1:T(8,128)S(1)}, u32[]{:S(2)}, u32[]{:S(2)}) async-start(f32[8,32,512]{2,0,1:T(8,128)} %copy.32), calls=%async_computation | async-start | bytes 1048576 | tf_op jit(solution)/shard_map/all_to_all | solution.py:93
  38.7 20.4 %all-to-all-done = f32[8,32,512]{2,0,1:T(8,128)S(1)} async-done(((f32[8,32,512]{2,0,1:T(8,128)}), f32[8,32,512]{2,0,1:T(8,128)S(1)}, u32[]{:S(2)}, u32[]{:S(2)}) %all-to-all-start) | async-done | bytes 524320 | tf_op jit(solution)/shard_map/all_to_all | solution.py:93
  59.2 0.3 reshape.64
  59.5 0.1 reduce_sum.18
  59.7 0.0 copy-start.3
  59.7 0.2 copy.35
  59.9 0.3 copy-done.2
  60.3 0.3 fusion.53
  60.6 0.3 fusion.52
  60.9 0.1 subtract_multiply_fusion
  61.0 0.8 multiply_reduce_fusion
  61.8 0.7 fusion.4
  62.6 0.7 fusion.69
  63.3 0.6 fusion.54
  63.9 0.7 fusion.3
  64.6 0.7 fusion.78
  65.2 0.7 fusion.77
  65.9 0.7 fusion.2
  66.5 0.7 fusion.80
  67.2 0.7 fusion.79
  67.9 0.3 fusion.81
  68.1 0.7 fusion.1
  68.8 0.7 convolution_divide_fusion
  69.5 0.5 fusion.65
  70.0 0.6 fusion.63
  70.6 0.8 fusion
  71.3 0.2 copy.36
  71.6 0.4 all_to_all.27
  72.0 26.0 %all_to_all.32 = f32[32,8,512]{2,1,0:T(8,128)S(1)} all-to-all(f32[32,8,512]{2,1,0:T(8,128)S(1)} %all_to_all.27), channel_id=1, replica_groups=mesh['mem'=32,'strip'=32] {'mem'}, dimensions={0} | all-to-all | bytes 1048576 | tf_op jit(solution)/shard_map/all_to_all | solution.py:97
  98.0 0.3 copy.37
  98.3 1.0 %reshape.65 = f32[8,8,2048]{2,1,0:T(8,128)} reshape(f32[8,32,512]{2,1,0:T(8,128)S(1)} %copy.37) | data formatting | bytes 1048576 | tf_op jit(solution)/shard_map/reshape | solution.py:98
  (25 shorter events, 0.2 us)
Async XLA Ops:
  1.7 15.6 %collective-permute-start = (f32[9,4,2048]{2,0,1:T(8,128)S(1)}, f32[9,4,2048]{2,0,1:T(8,128)S(1)}, u32[]{:S(2)}, u32[]{:S(2)}) collective-permute-start(f32[9,4,2048]{2,0,1:T(8,128)S(1)} %copy.28), channel_id=1, source_target_pairs={{0,1},{1,2},{2,3},{3,4},{4,5},{5,6},{6,7},{7,8},{8,9},{9,10},{10,1... | collective-permute-start | bytes 884744 | tf_op jit(solution)/shard_map/ppermute | solution.py:22
  3.6 14.1 %copy-start = (f32[8,8,2048]{2,1,0:T(8,128)S(1)}, f32[8,8,2048]{2,1,0:T(8,128)}, u32[]{:S(2)}) copy-start(f32[8,8,2048]{2,1,0:T(8,128)} %param.6) | copy-start | bytes 1572868
  3.6 14.1 %copy-start.1 = (f32[8,2048]{1,0:T(8,128)S(1)}, f32[8,2048]{1,0:T(8,128)}, u32[]{:S(2)}) copy-start(f32[8,2048]{1,0:T(8,128)} %param.7) | copy-start | bytes 196612
  3.8 13.7 %collective-permute-start.1 = (f32[9,4,2048]{2,0,1:T(8,128)S(1)}, f32[9,4,2048]{2,0,1:T(8,128)S(1)}, u32[]{:S(2)}, u32[]{:S(2)}) collective-permute-start(f32[9,4,2048]{2,0,1:T(8,128)S(1)} %copy.29), channel_id=1, source_target_pairs={{1,0},{2,1},{3,2},{4,3},{5,4},{6,5},{7,6},{8,7},{9,8},{10,9},{11,1... | collective-permute-start | bytes 884744 | tf_op jit(solution)/shard_map/ppermute | solution.py:25
  24.6 34.6 %all-to-all-start = ((f32[8,32,512]{2,0,1:T(8,128)}), f32[8,32,512]{2,0,1:T(8,128)S(1)}, u32[]{:S(2)}, u32[]{:S(2)}) async-start(f32[8,32,512]{2,0,1:T(8,128)} %copy.32), calls=%async_computation | async-start | bytes 1048576 | tf_op jit(solution)/shard_map/all_to_all | solution.py:93
  59.6 0.7 copy-start.2
  59.7 1.2 %copy-start.3 = (f32[2,128]{1,0:T(2,128)S(1)}, f32[2,128]{1,0:T(2,128)}, u32[]{:S(2)}) copy-start(f32[2,128]{1,0:T(2,128)} %param.10) | copy-start | bytes 3076
  59.7 1.2 %copy-start.4 = (f32[2,128]{1,0:T(2,128)S(1)}, f32[2,128]{1,0:T(2,128)}, u32[]{:S(2)}) copy-start(f32[2,128]{1,0:T(2,128)} %param.11) | copy-start | bytes 3076
  59.7 1.2 %copy-start.5 = (s32[2]{0:T(128)S(1)}, s32[2]{0:T(128)}, u32[]{:S(2)}) copy-start(s32[2]{0:T(128)} %param.9) | copy-start | bytes 28
where the time goes:
time: 99.6 us; the launch traced here: 99.3 us
  waiting for transfers between devices  29.1 us (29%)
  blocking collectives  26 us (26%)
  starting transfers between devices  20.5 us (21%)
  matrix products  10.8 us (11%)
  local copies, waits for them, and re-layouts  7.55 us (8%)
  other arithmetic  4.88 us (5%)
    all_to_all x1, blocking collectives, local(): lax.all_to_all(analysis, 'mem', split_axis=0, concat_axis=1, tiled=True)  26 us
    all_to_all x1, waiting for transfers between devices, local(): lax.all_to_all(flat_state, 'mem', split_axis=1, concat_axis=0, tiled=True)  20.4 us
    all_to_all x1, starting transfers between devices, local(): lax.all_to_all(flat_state, 'mem', split_axis=1, concat_axis=0, tiled=True)  14.1 us
    ppermute x1, waiting for transfers between devices, padded(): lax.ppermute(lax.slice_in_dim(block, block.shape[dim] - width, None, axis...  8.62 us
    ppermute x1, starting transfers between devices, padded(): lax.ppermute(lax.slice_in_dim(block, 0, width, axis=dim), axis, backward)  4.54 us
    mul x4, other arithmetic, local(): advanced * inside[sweep_index + 1:sweep_index + 1 + rows_next][None, :, N...  2.96 us
    dot_general x4, matrix products, analyze(): jnp.einsum('rij,rjk->rik', right_iterate, left_iterate, precision=highest)  2.7 us
    dot_general x4, matrix products, analyze(): jnp.einsum('rij,rjk->rik', correction, right_iterate, precision=highest)  2.59 us
  transfers between devices with their start and end apart: 3, of which 2 were waited for; matrix products, arithmetic and copies ran while one was open for 1% of the time, Pallas kernels for 0%

commit v1 on v0

v1 whole, which is shorter than its diff:
```python
import functools
import math

import jax
import jax.numpy as jnp
from jax import lax
from jax.experimental import pallas as pl
from jax.experimental.pallas import tpu as pltpu
from jax.sharding import PartitionSpec as P


STEPS = 4
NS_ITERS = 4
REGION_VALUES = 256

step_size = 0.05
coupling = 0.4

VMEM = pl.BlockSpec(memory_space=pltpu.VMEM)
ANY = pl.BlockSpec(memory_space=pl.ANY)
SMEM = pl.BlockSpec(memory_space=pltpu.SMEM)
GRANT = 16 * 1024 * 1024


def params():
    return pltpu.CompilerParams(vmem_limit_bytes=GRANT)


def pack_kernel(strip_ref, ens_ref, forcing_ref, cross_ref, near_ref):
    odd = lax.rem(strip_ref[0], 2)
    for parity, low, high in ((0, cross_ref, near_ref), (1, near_ref, cross_ref)):

        @pl.when(odd == parity)
        def _():
            for row in range(STEPS):
                low[row] = ens_ref[:, row, :]
                high[row] = ens_ref[:, STEPS + row, :]

    cross_ref[STEPS] = forcing_ref[...]
    near_ref[STEPS] = forcing_ref[...]


def columns_kernel(count_ref, index_ref, value_ref, precision_ref, after_ref, columns_ref):
    slots = index_ref.shape[1]
    slot = lax.broadcasted_iota(jnp.int32, (1, slots), 1)
    lines = []
    for region in range(index_ref.shape[0]):
        live = (slot < count_ref[region]).astype(jnp.float32)
        weight = precision_ref[region : region + 1, :] * live
        lines += [
            index_ref[region : region + 1, :].astype(jnp.float32),
            jnp.sqrt(weight),
            value_ref[region : region + 1, :],
            weight,
        ]
    columns_ref[...] = jnp.concatenate(lines, axis=0).T


def forecast_kernel(last, strip_ref, after_ref, own_near_ref, own_cross_ref, got_near_ref, got_cross_ref, out_ref, even_ref, other_ref, forcing_ref):
    strip = strip_ref[0]
    odd = lax.rem(strip, 2)
    rows = 2 * STEPS
    lon = out_ref.shape[0] * out_ref.shape[2] // rows
    own_cross_at = STEPS + STEPS * odd
    own_near_at = 2 * STEPS - STEPS * odd
    got_cross_at = 3 * STEPS * odd
    got_near_at = 3 * STEPS - 3 * STEPS * odd
    for row in range(STEPS):
        even_ref[own_cross_at + row] = own_cross_ref[row]
        even_ref[own_near_at + row] = own_near_ref[row]
        even_ref[got_cross_at + row] = got_cross_ref[row]
        even_ref[got_near_at + row] = got_near_ref[row]
    forcing_ref[1] = own_near_ref[STEPS]
    forcing_ref[2 * odd] = got_cross_ref[STEPS]
    forcing_ref[2 - 2 * odd] = got_near_ref[STEPS]
    buffers = (even_ref, other_ref)
    for step in range(STEPS):
        source, target = buffers[step % 2], buffers[(step + 1) % 2]
        final = step == STEPS - 1

        def advance(row, carry):
            center = source[row]
            around = source[row - 1] + source[row + 1]
            far = row + rows - STEPS
            force = forcing_ref[far // rows, pl.ds(lax.rem(far, rows), 1), :]
            west = pltpu.roll(center, 1, 1)
            west2 = pltpu.roll(center, 2, 1)
            east = pltpu.roll(center, lon - 1, 1)
            new = (
                center * (1.0 - step_size - 2.0 * coupling)
                + step_size * ((east - west2) * west + force)
                + coupling * around
            )
            if final:
                parts = lon // out_ref.shape[2]
                for part in range(parts):
                    out_ref[(row - STEPS) * parts + part] = new[:, part * out_ref.shape[2] : (part + 1) * out_ref.shape[2]]
            else:
                below = jnp.logical_and(row < STEPS, strip == 0)
                above = jnp.logical_and(row >= STEPS + rows, strip == last)
                outside = jnp.logical_or(below, above)
                target[row] = new * jnp.where(outside, 0.0, 1.0)
            return carry

        lax.fori_loop(step + 1, rows + 2 * STEPS - 1 - step, advance, 0)


def halves(x):
    high = x.astype(jnp.bfloat16)
    return high, (x - high.astype(jnp.float32)).astype(jnp.bfloat16)


NN = (((1,), (0,)), ((), ()))
NT = (((1,), (1,)), ((), ()))


def dot(a, b, dims):
    return lax.dot_general(a, b, dims, preferred_element_type=jnp.float32)


def product(a, b, dims=NN):
    (ah, al), (bh, bl) = a, b
    return dot(ah, bh, dims) + (dot(ah, bl, dims) + dot(al, bh, dims))


def analysis_kernel(columns_ref, block_ref, out_ref):
    chunks, per, _ = block_ref.shape
    members = chunks * per
    slots = columns_ref.shape[0]
    regions = block_ref.shape[2] // REGION_VALUES
    top = members - 1.0
    columns = columns_ref[...]
    for region in range(regions):
        cells = slice(region * REGION_VALUES, (region + 1) * REGION_VALUES)
        block = block_ref[:, :, cells].reshape(members, REGION_VALUES)
        index, root, value, _ = (columns[:, 4 * region + i : 4 * region + i + 1] for i in range(4))
        mean = jnp.sum(block, axis=0, keepdims=True) * (1.0 / members)
        spread = block - mean
        spread_parts = halves(spread)
        cell = lax.broadcasted_iota(jnp.int32, (slots, REGION_VALUES), 1).astype(jnp.float32)
        chosen = cell == index
        onehot = chosen.astype(jnp.bfloat16)
        observed = dot(onehot, spread_parts[0], NT) + dot(onehot, spread_parts[1], NT)
        obs_mean = jnp.sum(jnp.where(chosen, mean, 0.0), axis=1, keepdims=True)
        scaled = observed * root
        misfit = root * (value - obs_mean)
        scaled_parts = halves(scaled)
        small = product(scaled_parts, scaled_parts, NT)
        carried = product(scaled_parts, spread_parts)
        norm = top + jnp.sqrt(jnp.sum(small * small, keepdims=True))
        inverse = 1.0 / norm
        eye = (
            lax.broadcasted_iota(jnp.int32, (slots, slots), 0)
            == lax.broadcasted_iota(jnp.int32, (slots, slots), 1)
        ).astype(jnp.float32)
        left = (top * eye + small) * inverse
        left_zero = top * inverse
        left_rest = inverse * eye
        right = right_rest = None
        right_zero = jnp.ones_like(norm)
        for repeat in range(NS_ITERS):
            fix = 1.5 * eye - 0.5 * left
            fix_zero = 1.5 - 0.5 * left_zero
            fix_parts = halves(fix)
            if repeat == 0:
                right, right_rest = fix, -0.5 * left_rest
            else:
                new_rest = -0.5 * right_zero * left_rest
                if repeat == 1:
                    right_rest = (-0.5 * inverse) * fix + new_rest
                else:
                    right_rest = product(halves(right_rest), fix_parts) + new_rest
                right = product(halves(right), fix_parts)
            right_zero = right_zero * fix_zero
            if repeat < NS_ITERS - 1:
                square = product(fix_parts, fix_parts)
                mixed = square - (0.5 * left_zero) * (fix + fix_zero * eye)
                if repeat == 0:
                    left_rest = inverse * mixed
                else:
                    left_rest = product(halves(left_rest), halves(mixed))
                left = product(halves(left), halves(square))
                left_zero = left_zero * fix_zero * fix_zero
        along = jnp.sum(right * misfit, axis=0, keepdims=True)
        twice = jnp.sum(right * along, axis=1, keepdims=True)
        moved = jnp.sum(twice * carried, axis=0, keepdims=True) * inverse
        pushed = product(halves(right_rest), halves(carried))
        gain = math.sqrt(top) * lax.rsqrt(norm)
        turned = halves(scaled.T)
        update = product(turned, halves(pushed))
        result = (mean + moved) + gain * (right_zero * spread + update)
        out_ref[:, :, cells] = result.reshape(chunks, per, REGION_VALUES)


def unpack_kernel(block_ref, out_ref):
    rows = out_ref.shape[1]
    parts = block_ref.shape[0] // rows
    width = block_ref.shape[2]
    for row in range(rows):
        for part in range(parts):
            out_ref[:, row, part * width : (part + 1) * width] = block_ref[row * parts + part]


def local(ensemble, forcing, obs_index, obs_count, obs_value, obs_precision):
    per, rows, lon = ensemble.shape
    strips = lax.axis_size("strip")
    strip = lax.axis_index("strip").astype(jnp.int32).reshape(1)
    regions, slots = obs_index.shape
    slab = jax.ShapeDtypeStruct((STEPS + 1, per, lon), jnp.float32)

    cross, near = pl.pallas_call(
        pack_kernel,
        out_shape=(slab, slab),
        in_specs=[SMEM, VMEM, VMEM],
        out_specs=(VMEM, VMEM),
        compiler_params=params(),
        name="pack",
    )(strip, ensemble, forcing)
    span = [(i, i + 1) for i in range(1, strips - 1, 2)]
    span = span + [(b, a) for a, b in span]
    swap = [(i, i ^ 1) for i in range(strips)]
    got_cross = lax.ppermute(cross, "strip", span)
    got_near = lax.ppermute(near, "strip", swap)
    columns = pl.pallas_call(
        columns_kernel,
        out_shape=jax.ShapeDtypeStruct((slots, 4 * regions), jnp.float32),
        in_specs=[SMEM] + [VMEM] * 3 + [ANY],
        out_specs=VMEM,
        compiler_params=params(),
        cost_estimate=pl.CostEstimate(flops=10**7, bytes_accessed=4096, transcendentals=0),
        name="columns",
    )(obs_count, obs_index, obs_value, obs_precision, near)
    chunks = lax.axis_size("mem")
    width = rows * lon // chunks
    sent = pl.pallas_call(
        functools.partial(forecast_kernel, strips - 1),
        out_shape=jax.ShapeDtypeStruct((chunks, per, width), jnp.float32),
        in_specs=[SMEM, ANY] + [VMEM] * 4,
        out_specs=VMEM,
        scratch_shapes=[
            pltpu.VMEM((4 * STEPS, per, lon), jnp.float32),
            pltpu.VMEM((4 * STEPS, per, lon), jnp.float32),
            pltpu.VMEM((3, rows, lon), jnp.float32),
        ],
        compiler_params=params(),
        name="forecast",
    )(strip, columns, near, cross, got_near, got_cross)
    regional = lax.all_to_all(sent, "mem", split_axis=0, concat_axis=0, tiled=True)
    analysed = pl.pallas_call(
        analysis_kernel,
        out_shape=jax.ShapeDtypeStruct((chunks, per, width), jnp.float32),
        in_specs=[VMEM] * 2,
        out_specs=VMEM,
        compiler_params=params(),
        name="analysis",
    )(columns, regional)
    back = lax.all_to_all(analysed, "mem", split_axis=0, concat_axis=0, tiled=True)
    return pl.pallas_call(
        unpack_kernel,
        out_shape=jax.ShapeDtypeStruct((per, rows, lon), jnp.float32),
        in_specs=[VMEM],
        out_specs=VMEM,
        compiler_params=params(),
        name="unpack",
    )(back)


def solution(mesh):
    placed = (
        P("mem", "strip", None),
        P("strip", None),
        P(("strip", "mem"), None),
        P(("strip", "mem")),
        P(("strip", "mem"), None),
        P(("strip", "mem"), None),
    )
    return jax.shard_map(
        local, mesh=mesh, in_specs=placed, out_specs=P("mem", "strip", None), check_vma=False
    )
```

time: 99.6 us -> 83.6 us (0.84)
  the two profiles are of different devices: /device:TPU:258 before, /device:TPU:786 now
where the time goes in v1:
time: 83.6 us; the launch traced here: 83.3 us
  blocking collectives  58.6 us (70%)
  Pallas kernels  12.3 us (15%)
  starting transfers between devices  6.22 us (7%)
  waiting for transfers between devices  4.2 us (5%)
  local copies, waits for them, and re-layouts  1.91 us (2%)
    all_to_all x1, blocking collectives, local(): lax.all_to_all(sent, 'mem', split_axis=0, concat_axis=0, tiled=True)  33.6 us
    all_to_all x1, blocking collectives, local(): lax.all_to_all(analysed, 'mem', split_axis=0, concat_axis=0, tiled=True)  25 us
    pallas_call x1, Pallas kernels, local(): pl.pallas_call(functools.partial(forecast_kernel, strips - 1), out_shape=...  5.65 us
    pallas_call x1, Pallas kernels, local(): pl.pallas_call(analysis_kernel, out_shape=jax.ShapeDtypeStruct((chunks, p...  4.9 us
    ppermute x1, waiting for transfers between devices, local(): got_cross = lax.ppermute(cross, 'strip', span)  4.19 us
    ppermute x1, starting transfers between devices, local(): got_near = lax.ppermute(near, 'strip', swap)  4.17 us
    ppermute x1, starting transfers between devices, local(): got_cross = lax.ppermute(cross, 'strip', span)  2.05 us
    unnamed x12, local copies, waits for them, and re-layouts  1.91 us
  transfers between devices with their start and end apart: 2, of which 1 were waited for; matrix products, arithmetic and copies ran while one was open for 0% of the time, Pallas kernels for 1%

profile of v1, /device:TPU:786, one launch (start us, length us, event | category | flops | bytes accessed | tf_op | source)
XLA Modules:
  0.0 83.3 jit_solution(7088260749774754676)
XLA Ops:
  0.0 0.0 copy-start
  0.0 1.0 %copy-done = f32[8,8,2048]{2,1,0:T(8,128)S(1)} copy-done((f32[8,8,2048]{2,1,0:T(8,128)S(1)}, f32[8,8,2048]{2,1,0:T(8,128)}, u32[]{:S(2)}) %copy-start) | copy-done | bytes 524312
  1.0 0.0 copy-start.1
  1.0 0.8 %copy-done.1 = f32[8,2048]{1,0:T(8,128)S(1)} copy-done((f32[8,2048]{1,0:T(8,128)S(1)}, f32[8,2048]{1,0:T(8,128)}, u32[]{:S(2)}) %copy-start.1) | copy-done | bytes 65560
  1.9 0.1 pack.1
  2.0 0.0 copy-start.3
  2.0 0.0 copy-start.4
  2.0 0.0 copy-start.2
  2.1 0.0 copy-start.5
  2.1 2.1 %collective-permute-start.1 = (f32[5,8,2048]{2,1,0:T(8,128)S(1)}, f32[5,8,2048]{2,1,0:T(8,128)S(1)}, u32[]{:S(2)}, u32[]{:S(2)}) collective-permute-start(f32[5,8,2048]{2,1,0:T(8,128)S(1)} %get-tuple-element.8.own_cross_ref), channel_id=1, source_target_pairs={{1,2},{3,4},{5,6},{7,8},{9,10},{11,12},{13,14},{15,16},{17,18},{19... | collective-permute-start | bytes 983048 | tf_op jit(solution)/shard_map/ppermute | solution.py:222
  4.1 4.2 %collective-permute-start = (f32[5,8,2048]{2,1,0:T(8,128)S(1)}, f32[5,8,2048]{2,1,0:T(8,128)S(1)}, u32[]{:S(2)}, u32[]{:S(2)}) collective-permute-start(f32[5,8,2048]{2,1,0:T(8,128)S(1)} %get-tuple-element.7.after_ref.own_near_ref), channel_id=1, source_target_pairs={{0,1},{1,0},{2,3},{3,2},{4,5},{5,4},{6,7},{7,6},{8,9},{9,8},{10,11... | collective-permute-start | bytes 983048 | tf_op jit(solution)/shard_map/ppermute | solution.py:223
  8.3 0.0 copy-done.3
  8.3 0.0 copy-done.4
  8.3 0.0 copy-done.2
  8.3 0.0 copy-done.5
  8.3 0.7 columns.1.after_ref.columns_ref
  9.0 4.2 %collective-permute-done.1.got_cross_ref = f32[5,8,2048]{2,1,0:T(8,128)S(1)} collective-permute-done((f32[5,8,2048]{2,1,0:T(8,128)S(1)}, f32[5,8,2048]{2,1,0:T(8,128)S(1)}, u32[]{:S(2)}, u32[]{:S(2)}) %collective-permute-start.1) | collective-permute-done | bytes 327712 | tf_op jit(solution)/shard_map/ppermute | solution.py:222
  13.2 0.0 collective-permute-done.got_near_ref
  13.2 5.7 %forecast.1 = f32[32,8,512]{2,1,0:T(8,128)S(1)} custom-call(s32[1]{0:T(128)} %bitcast.strip_ref, f32[128,8]{1,0:T(8,128)S(1)} %columns.1.after_ref.columns_ref, f32[5,8,2048]{2,1,0:T(8,128)S(1)} %get-tuple-element.7.after_ref.own_near_ref, f32[5,8,2048]{2,1,0:T(8,128)S(1)} %get-tuple-element.8.own_cross_ref, ...), custom_call_target="tpu_custom_call" | custom-call | tf_op jit(solution)/shard_map/forecast/pallas_call | solution.py:235
  18.9 33.6 %all_to_all.10.block_ref = f32[32,8,512]{2,1,0:T(8,128)S(1)} all-to-all(f32[32,8,512]{2,1,0:T(8,128)S(1)} %forecast.1), channel_id=1, replica_groups=mesh['mem'=32,'strip'=32] {'mem'}, dimensions={0} | all-to-all | bytes 1048576 | tf_op jit(solution)/shard_map/all_to_all | solution.py:248
  52.5 4.9 %analysis.1 = f32[32,8,512]{2,1,0:T(8,128)S(1)} custom-call(f32[128,8]{1,0:T(8,128)S(1)} %columns.1.after_ref.columns_ref, f32[32,8,512]{2,1,0:T(8,128)S(1)} %all_to_all.10.block_ref), custom_call_target="tpu_custom_call" | custom-call | tf_op jit(solution)/shard_map/analysis/pallas_call | solution.py:249
  57.4 25.0 %all_to_all.11.block_ref = f32[32,8,512]{2,1,0:T(8,128)S(1)} all-to-all(f32[32,8,512]{2,1,0:T(8,128)S(1)} %analysis.1), channel_id=1, replica_groups=mesh['mem'=32,'strip'=32] {'mem'}, dimensions={0} | all-to-all | bytes 1048576 | tf_op jit(solution)/shard_map/all_to_all | solution.py:257
  82.3 0.9 %unpack.1 = f32[8,8,2048]{2,1,0:T(8,128)} custom-call(f32[32,8,512]{2,1,0:T(8,128)S(1)} %all_to_all.11.block_ref), custom_call_target="tpu_custom_call" | custom-call | tf_op jit(solution)/shard_map/unpack/pallas_call | solution.py:258
Async XLA Ops:
  0.0 1.0 %copy-start = (f32[8,8,2048]{2,1,0:T(8,128)S(1)}, f32[8,8,2048]{2,1,0:T(8,128)}, u32[]{:S(2)}) copy-start(f32[8,8,2048]{2,1,0:T(8,128)} %ens_ref.1) | copy-start | bytes 1572868
  1.0 0.8 %copy-start.1 = (f32[8,2048]{1,0:T(8,128)S(1)}, f32[8,2048]{1,0:T(8,128)}, u32[]{:S(2)}) copy-start(f32[8,2048]{1,0:T(8,128)} %forcing_ref.1) | copy-start | bytes 196612
  2.0 6.3 %copy-start.3 = (f32[2,128]{1,0:T(2,128)S(1)}, f32[2,128]{1,0:T(2,128)}, u32[]{:S(2)}) copy-start(f32[2,128]{1,0:T(2,128)} %value_ref.1) | copy-start | bytes 3076
  2.0 6.3 %copy-start.4 = (f32[2,128]{1,0:T(2,128)S(1)}, f32[2,128]{1,0:T(2,128)}, u32[]{:S(2)}) copy-start(f32[2,128]{1,0:T(2,128)} %precision_ref.1) | copy-start | bytes 3076
  2.0 6.3 %copy-start.2 = (s32[2,128]{1,0:T(2,128)S(1)}, s32[2,128]{1,0:T(2,128)}, u32[]{:S(2)}) copy-start(s32[2,128]{1,0:T(2,128)} %index_ref.1) | copy-start | bytes 3076
  2.1 6.3 %copy-start.5 = (s32[2]{0:T(128)S(1)}, s32[2]{0:T(128)}, u32[]{:S(2)}) copy-start(s32[2]{0:T(128)} %count_ref.1) | copy-start | bytes 28
  2.1 11.1 %collective-permute-start.1 = (f32[5,8,2048]{2,1,0:T(8,128)S(1)}, f32[5,8,2048]{2,1,0:T(8,128)S(1)}, u32[]{:S(2)}, u32[]{:S(2)}) collective-permute-start(f32[5,8,2048]{2,1,0:T(8,128)S(1)} %get-tuple-element.8.own_cross_ref), channel_id=1, source_target_pairs={{1,2},{3,4},{5,6},{7,8},{9,10},{11,12},{13,14},{15,16},{17,18},{19... | collective-permute-start | bytes 983048 | tf_op jit(solution)/shard_map/ppermute | solution.py:222
  4.1 9.1 %collective-permute-start = (f32[5,8,2048]{2,1,0:T(8,128)S(1)}, f32[5,8,2048]{2,1,0:T(8,128)S(1)}, u32[]{:S(2)}, u32[]{:S(2)}) collective-permute-start(f32[5,8,2048]{2,1,0:T(8,128)S(1)} %get-tuple-element.7.after_ref.own_near_ref), channel_id=1, source_target_pairs={{0,1},{1,0},{2,3},{3,2},{4,5},{5,4},{6,7},{7,6},{8,9},{9,8},{10,11... | collective-permute-start | bytes 983048 | tf_op jit(solution)/shard_map/ppermute | solution.py:223

commit v2 on v1

--- a/solution.py
+++ b/solution.py
@@ -73,16 +73,18 @@
     forcing_ref[1] = own_near_ref[STEPS]
     forcing_ref[2 * odd] = got_cross_ref[STEPS]
     forcing_ref[2 - 2 * odd] = got_near_ref[STEPS]
+    low_kept = jnp.where(strip == 0, 0.0, 1.0)
+    high_kept = jnp.where(strip == last, 0.0, 1.0)
     buffers = (even_ref, other_ref)
     for step in range(STEPS):
         source, target = buffers[step % 2], buffers[(step + 1) % 2]
         final = step == STEPS - 1
 
-        def advance(row, carry):
+        for row in range(step + 1, rows + 2 * STEPS - 1 - step):
             center = source[row]
             around = source[row - 1] + source[row + 1]
             far = row + rows - STEPS
-            force = forcing_ref[far // rows, pl.ds(lax.rem(far, rows), 1), :]
+            force = forcing_ref[far // rows, far % rows : far % rows + 1, :]
             west = pltpu.roll(center, 1, 1)
             west2 = pltpu.roll(center, 2, 1)
             east = pltpu.roll(center, lon - 1, 1)
@@ -92,17 +94,20 @@
                 + coupling * around
             )
             if final:
-                parts = lon // out_ref.shape[2]
+                width = out_ref.shape[2]
+                parts = lon // width
                 for part in range(parts):
-                    out_ref[(row - STEPS) * parts + part] = new[:, part * out_ref.shape[2] : (part + 1) * out_ref.shape[2]]
+                    out_ref[(row - STEPS) * parts + part] = new[:, part * width : (part + 1) * width]
+            elif row < STEPS:
+                target[row] = new * low_kept
+            elif row >= STEPS + rows:
+                target[row] = new * high_kept
             else:
-                below = jnp.logical_and(row < STEPS, strip == 0)
-                above = jnp.logical_and(row >= STEPS + rows, strip == last)
-                outside = jnp.logical_or(below, above)
-                target[row] = new * jnp.where(outside, 0.0, 1.0)
-            return carry
-
-        lax.fori_loop(step + 1, rows + 2 * STEPS - 1 - step, advance, 0)
+                target[row] = new
+
+
+NN = (((1,), (0,)), ((), ()))
+NT = (((1,), (1,)), ((), ()))
 
 
 def halves(x):
@@ -110,17 +115,26 @@
     return high, (x - high.astype(jnp.float32)).astype(jnp.bfloat16)
 
 
-NN = (((1,), (0,)), ((), ()))
-NT = (((1,), (1,)), ((), ()))
-
-
-def dot(a, b, dims):
+def dot(a, b, dims=NN):
     return lax.dot_general(a, b, dims, preferred_element_type=jnp.float32)
 
 
-def product(a, b, dims=NN):
-    (ah, al), (bh, bl) = a, b
-    return dot(ah, bh, dims) + (dot(ah, bl, dims) + dot(al, bh, dims))
+def across(parts):
+    high, low = parts
+    return jnp.concatenate([high, low, high], axis=1)
+
+
+def down(parts):
+    high, low = parts
+    return jnp.concatenate([high, high, low], axis=0)
+
+
+def stack(*parts):
+    return tuple(jnp.concatenate(p, axis=0) for p in zip(*parts))
+
+
+def product(a, b):
+    return dot(across(a), down(b))
 
 
 def analysis_kernel(columns_ref, block_ref, out_ref):
@@ -130,66 +144,88 @@
     regions = block_ref.shape[2] // REGION_VALUES
     top = members - 1.0
     columns = columns_ref[...]
-    for region in range(regions):
-        cells = slice(region * REGION_VALUES, (region + 1) * REGION_VALUES)
+    eye = (lax.broadcasted_iota(jnp.int32, (slots, slots), 0) == lax.broadcasted_iota(jnp.int32, (slots, slots), 1)).astype(jnp.float32)
+    cell = lax.broadcasted_iota(jnp.int32, (slots, REGION_VALUES), 1).astype(jnp.float32)
+
+    def begin(r):
+        cells = slice(r * REGION_VALUES, (r + 1) * REGION_VALUES)
         block = block_ref[:, :, cells].reshape(members, REGION_VALUES)
-        index, root, value, _ = (columns[:, 4 * region + i : 4 * region + i + 1] for i in range(4))
+        index, root, value = (columns[:, 4 * r + i : 4 * r + i + 1] for i in range(3))
         mean = jnp.sum(block, axis=0, keepdims=True) * (1.0 / members)
         spread = block - mean
-        spread_parts = halves(spread)
-        cell = lax.broadcasted_iota(jnp.int32, (slots, REGION_VALUES), 1).astype(jnp.float32)
+        sh, sl = halves(spread)
         chosen = cell == index
         onehot = chosen.astype(jnp.bfloat16)
-        observed = dot(onehot, spread_parts[0], NT) + dot(onehot, spread_parts[1], NT)
+        observed = dot(onehot, sh, NT) + dot(onehot, sl, NT)
         obs_mean = jnp.sum(jnp.where(chosen, mean, 0.0), axis=1, keepdims=True)
         scaled = observed * root
         misfit = root * (value - obs_mean)
-        scaled_parts = halves(scaled)
-        small = product(scaled_parts, scaled_parts, NT)
-        carried = product(scaled_parts, spread_parts)
+        gh, gl = halves(scaled)
+        small = dot(jnp.concatenate([gh, gl, gh], axis=1), jnp.concatenate([gh, gh, gl], axis=1), NT)
+        carried = product((gh, gl), (sh, sl))
         norm = top + jnp.sqrt(jnp.sum(small * small, keepdims=True))
         inverse = 1.0 / norm
-        eye = (
-            lax.broadcasted_iota(jnp.int32, (slots, slots), 0)
-            == lax.broadcasted_iota(jnp.int32, (slots, slots), 1)
-        ).astype(jnp.float32)
-        left = (top * eye + small) * inverse
+        return dict(mean=mean, scaled=scaled, misfit=misfit, carried=carried, norm=norm, inverse=inverse, small=small)
+
+    def iterate(s):
+        inverse = s["inverse"]
+        left = (top * inverse) * eye + s["small"] * inverse
         left_zero = top * inverse
-        left_rest = inverse * eye
-        right = right_rest = None
-        right_zero = jnp.ones_like(norm)
-        for repeat in range(NS_ITERS):
+        fix = 1.5 * eye - 0.5 * left
+        fix_zero = 1.5 - 0.5 * left_zero
+        f = halves(fix)
+        square = product(f, f)
+        yield 2
+        mixed = square - (0.5 * left_zero) * (fix + fix_zero * eye)
+        left_rest = inverse * mixed
+        left = product(halves(left), halves(square))
+        yield 2
+        right, right_zero, rest = fix, fix_zero, (-0.5 * inverse) * eye
+        left_zero = left_zero * fix_zero * fix_zero
+        for repeat in range(1, NS_ITERS):
             fix = 1.5 * eye - 0.5 * left
             fix_zero = 1.5 - 0.5 * left_zero
-            fix_parts = halves(fix)
-            if repeat == 0:
-                right, right_rest = fix, -0.5 * left_rest
+            f = halves(fix)
+            last = repeat == NS_ITERS - 1
+            rows = [halves(right)] if last else [f, halves(right), halves(left_rest)]
+            if repeat > 1: rows.append(halves(rest))
+            got = product(stack(*rows), f)
+            got = [got[i * slots : (i + 1) * slots] for i in range(len(rows))]
+            yield 2
+            new_rest = (got[-1] if repeat > 1 else (-0.5 * inverse) * fix) - (0.5 * right_zero) * left_rest
+            if not last:
+                square, right, rest_fix = got[:3]
+                both = product(stack(halves(left), halves(left_rest)), halves(square))
+                left = both[:slots]
+                left_rest = both[slots:] - (0.5 * left_zero) * (rest_fix + fix_zero * left_rest)
+                left_zero = left_zero * fix_zero * fix_zero
+                yield 2
             else:
-                new_rest = -0.5 * right_zero * left_rest
-                if repeat == 1:
-                    right_rest = (-0.5 * inverse) * fix + new_rest
-                else:
-                    right_rest = product(halves(right_rest), fix_parts) + new_rest
-                right = product(halves(right), fix_parts)
+                right = got[0]
+            rest = new_rest
             right_zero = right_zero * fix_zero
-            if repeat < NS_ITERS - 1:
-                square = product(fix_parts, fix_parts)
-                mixed = square - (0.5 * left_zero) * (fix + fix_zero * eye)
-                if repeat == 0:
-                    left_rest = inverse * mixed
-                else:
-                    left_rest = product(halves(left_rest), halves(mixed))
-                left = product(halves(left), halves(square))
-                left_zero = left_zero * fix_zero * fix_zero
-        along = jnp.sum(right * misfit, axis=0, keepdims=True)
+        s.update(right=right, right_zero=right_zero, rest=rest)
+
+    def finish(r, s):
+        cells = slice(r * REGION_VALUES, (r + 1) * REGION_VALUES)
+        right, carried = s["right"], s["carried"]
+        along = jnp.sum(right * s["misfit"], axis=0, keepdims=True)
         twice = jnp.sum(right * along, axis=1, keepdims=True)
-        moved = jnp.sum(twice * carried, axis=0, keepdims=True) * inverse
-        pushed = product(halves(right_rest), halves(carried))
-        gain = math.sqrt(top) * lax.rsqrt(norm)
-        turned = halves(scaled.T)
-        update = product(turned, halves(pushed))
-        result = (mean + moved) + gain * (right_zero * spread + update)
+        moved = jnp.sum(twice * carried, axis=0, keepdims=True) * s["inverse"]
+        pushed = product(halves(s["rest"]), halves(carried))
+        gain = math.sqrt(top) * lax.rsqrt(s["norm"])
+        update = product(halves(s["scaled"].T * gain), halves(pushed))
+        block = block_ref[:, :, cells].reshape(members, REGION_VALUES)
+        keep = gain * s["right_zero"]
+        result = keep * block + (s["mean"] * (1.0 - keep) + moved) + update
         out_ref[:, :, cells] = result.reshape(chunks, per, REGION_VALUES)
+
+    states = [begin(r) for r in range(regions)]
+    runs = [iterate(s) for s in states]
+    while runs:
+        runs = [run for run in runs if next(run, 0)]
+    for r in range(regions):
+        finish(r, states[r])
 
 
 def unpack_kernel(block_ref, out_ref):
@@ -274,6 +310,4 @@
         P(("strip", "mem"), None),
         P(("strip", "mem"), None),
     )
-    return jax.shard_map(
-        local, mesh=mesh, in_specs=placed, out_specs=P("mem", "strip", None), check_vma=False
-    )
+    return jax.shard_map(local, mesh=mesh, in_specs=placed, out_specs=P("mem", "strip", None), check_vma=False)

time: 83.6 us -> 78.3 us (0.937)
  Pallas kernels: 12.3 us -> 7.05 us
    pallas_call x1, Pallas kernels: 5.65 us -> 2.68 us  [local(): pl.pallas_call(functools.partial(forecast_kernel, strips - 1), out_shape=...]
    pallas_call x1, Pallas kernels: 4.9 us -> 2.66 us  [local(): pl.pallas_call(analysis_kernel, out_shape=jax.ShapeDtypeStruct((chunks, p...]
where the time goes in v2:
time: 78.3 us; the launch traced here: 78 us
  blocking collectives  58.6 us (75%)
  Pallas kernels  7.05 us (9%)
  starting transfers between devices  6.22 us (8%)
  waiting for transfers between devices  4.2 us (5%)
  local copies, waits for them, and re-layouts  1.91 us (2%)
    all_to_all x1, blocking collectives, local(): lax.all_to_all(sent, 'mem', split_axis=0, concat_axis=0, tiled=True)  33.6 us
    all_to_all x1, blocking collectives, local(): lax.all_to_all(analysed, 'mem', split_axis=0, concat_axis=0, tiled=True)  24.9 us
    ppermute x1, waiting for transfers between devices, local(): got_cross = lax.ppermute(cross, 'strip', span)  4.19 us
    ppermute x1, starting transfers between devices, local(): got_near = lax.ppermute(near, 'strip', swap)  4.17 us
    pallas_call x1, Pallas kernels, local(): pl.pallas_call(functools.partial(forecast_kernel, strips - 1), out_shape=...  2.68 us
    pallas_call x1, Pallas kernels, local(): pl.pallas_call(analysis_kernel, out_shape=jax.ShapeDtypeStruct((chunks, p...  2.66 us
    ppermute x1, starting transfers between devices, local(): got_cross = lax.ppermute(cross, 'strip', span)  2.05 us
    unnamed x12, local copies, waits for them, and re-layouts  1.91 us
  transfers between devices with their start and end apart: 2, of which 1 were waited for; matrix products, arithmetic and copies ran while one was open for 0% of the time, Pallas kernels for 1%

profile of v2, /device:TPU:786, one launch (start us, length us, event | category | flops | bytes accessed | tf_op | source)
XLA Modules:
  0.0 78.0 jit_solution(13889513085165328017)
XLA Ops:
  0.0 0.0 copy-start
  0.0 1.0 %copy-done = f32[8,8,2048]{2,1,0:T(8,128)S(1)} copy-done((f32[8,8,2048]{2,1,0:T(8,128)S(1)}, f32[8,8,2048]{2,1,0:T(8,128)}, u32[]{:S(2)}) %copy-start) | copy-done | bytes 524312
  1.0 0.0 copy-start.1
  1.0 0.8 %copy-done.1 = f32[8,2048]{1,0:T(8,128)S(1)} copy-done((f32[8,2048]{1,0:T(8,128)S(1)}, f32[8,2048]{1,0:T(8,128)}, u32[]{:S(2)}) %copy-start.1) | copy-done | bytes 65560
  1.9 0.1 pack.1
  2.0 0.0 copy-start.3
  2.0 0.0 copy-start.4
  2.0 0.0 copy-start.2
  2.1 0.0 copy-start.5
  2.1 2.1 %collective-permute-start.1 = (f32[5,8,2048]{2,1,0:T(8,128)S(1)}, f32[5,8,2048]{2,1,0:T(8,128)S(1)}, u32[]{:S(2)}, u32[]{:S(2)}) collective-permute-start(f32[5,8,2048]{2,1,0:T(8,128)S(1)} %get-tuple-element.8.own_cross_ref), channel_id=1, source_target_pairs={{1,2},{3,4},{5,6},{7,8},{9,10},{11,12},{13,14},{15,16},{17,18},{19... | collective-permute-start | bytes 983048 | tf_op jit(solution)/shard_map/ppermute | solution.py:258
  4.1 4.2 %collective-permute-start = (f32[5,8,2048]{2,1,0:T(8,128)S(1)}, f32[5,8,2048]{2,1,0:T(8,128)S(1)}, u32[]{:S(2)}, u32[]{:S(2)}) collective-permute-start(f32[5,8,2048]{2,1,0:T(8,128)S(1)} %get-tuple-element.7.after_ref.own_near_ref), channel_id=1, source_target_pairs={{0,1},{1,0},{2,3},{3,2},{4,5},{5,4},{6,7},{7,6},{8,9},{9,8},{10,11... | collective-permute-start | bytes 983048 | tf_op jit(solution)/shard_map/ppermute | solution.py:259
  8.3 0.0 copy-done.3
  8.3 0.0 copy-done.4
  8.3 0.0 copy-done.2
  8.3 0.0 copy-done.5
  8.3 0.7 columns.1.after_ref.columns_ref
  9.0 4.2 %collective-permute-done.1.got_cross_ref = f32[5,8,2048]{2,1,0:T(8,128)S(1)} collective-permute-done((f32[5,8,2048]{2,1,0:T(8,128)S(1)}, f32[5,8,2048]{2,1,0:T(8,128)S(1)}, u32[]{:S(2)}, u32[]{:S(2)}) %collective-permute-start.1) | collective-permute-done | bytes 327712 | tf_op jit(solution)/shard_map/ppermute | solution.py:258
  13.2 0.0 collective-permute-done.got_near_ref
  13.2 2.7 %forecast.1 = f32[32,8,512]{2,1,0:T(8,128)S(1)} custom-call(s32[1]{0:T(128)} %bitcast.strip_ref, f32[128,8]{1,0:T(8,128)S(1)} %columns.1.after_ref.columns_ref, f32[5,8,2048]{2,1,0:T(8,128)S(1)} %get-tuple-element.7.after_ref.own_near_ref, f32[5,8,2048]{2,1,0:T(8,128)S(1)} %get-tuple-element.8.own_cross_ref, ...), custom_call_target="tpu_custom_call" | custom-call | tf_op jit(solution)/shard_map/forecast/pallas_call | solution.py:271
  15.9 33.6 %all_to_all.10.block_ref = f32[32,8,512]{2,1,0:T(8,128)S(1)} all-to-all(f32[32,8,512]{2,1,0:T(8,128)S(1)} %forecast.1), channel_id=1, replica_groups=mesh['mem'=32,'strip'=32] {'mem'}, dimensions={0} | all-to-all | bytes 1048576 | tf_op jit(solution)/shard_map/all_to_all | solution.py:284
  49.5 2.7 %analysis.1 = f32[32,8,512]{2,1,0:T(8,128)S(1)} custom-call(f32[128,8]{1,0:T(8,128)S(1)} %columns.1.after_ref.columns_ref, f32[32,8,512]{2,1,0:T(8,128)S(1)} %all_to_all.10.block_ref), custom_call_target="tpu_custom_call" | custom-call | tf_op jit(solution)/shard_map/analysis/pallas_call | solution.py:285
  52.2 24.9 %all_to_all.11.block_ref = f32[32,8,512]{2,1,0:T(8,128)S(1)} all-to-all(f32[32,8,512]{2,1,0:T(8,128)S(1)} %analysis.1), channel_id=1, replica_groups=mesh['mem'=32,'strip'=32] {'mem'}, dimensions={0} | all-to-all | bytes 1048576 | tf_op jit(solution)/shard_map/all_to_all | solution.py:293
  77.1 0.9 %unpack.1 = f32[8,8,2048]{2,1,0:T(8,128)} custom-call(f32[32,8,512]{2,1,0:T(8,128)S(1)} %all_to_all.11.block_ref), custom_call_target="tpu_custom_call" | custom-call | tf_op jit(solution)/shard_map/unpack/pallas_call | solution.py:294
Async XLA Ops:
  0.0 1.0 %copy-start = (f32[8,8,2048]{2,1,0:T(8,128)S(1)}, f32[8,8,2048]{2,1,0:T(8,128)}, u32[]{:S(2)}) copy-start(f32[8,8,2048]{2,1,0:T(8,128)} %ens_ref.1) | copy-start | bytes 1572868
  1.0 0.8 %copy-start.1 = (f32[8,2048]{1,0:T(8,128)S(1)}, f32[8,2048]{1,0:T(8,128)}, u32[]{:S(2)}) copy-start(f32[8,2048]{1,0:T(8,128)} %forcing_ref.1) | copy-start | bytes 196612
  2.0 6.3 %copy-start.3 = (f32[2,128]{1,0:T(2,128)S(1)}, f32[2,128]{1,0:T(2,128)}, u32[]{:S(2)}) copy-start(f32[2,128]{1,0:T(2,128)} %value_ref.1) | copy-start | bytes 3076
  2.0 6.3 %copy-start.4 = (f32[2,128]{1,0:T(2,128)S(1)}, f32[2,128]{1,0:T(2,128)}, u32[]{:S(2)}) copy-start(f32[2,128]{1,0:T(2,128)} %precision_ref.1) | copy-start | bytes 3076
  2.0 6.3 %copy-start.2 = (s32[2,128]{1,0:T(2,128)S(1)}, s32[2,128]{1,0:T(2,128)}, u32[]{:S(2)}) copy-start(s32[2,128]{1,0:T(2,128)} %index_ref.1) | copy-start | bytes 3076
  2.1 6.3 %copy-start.5 = (s32[2]{0:T(128)S(1)}, s32[2]{0:T(128)}, u32[]{:S(2)}) copy-start(s32[2]{0:T(128)} %count_ref.1) | copy-start | bytes 28
  2.1 11.1 %collective-permute-start.1 = (f32[5,8,2048]{2,1,0:T(8,128)S(1)}, f32[5,8,2048]{2,1,0:T(8,128)S(1)}, u32[]{:S(2)}, u32[]{:S(2)}) collective-permute-start(f32[5,8,2048]{2,1,0:T(8,128)S(1)} %get-tuple-element.8.own_cross_ref), channel_id=1, source_target_pairs={{1,2},{3,4},{5,6},{7,8},{9,10},{11,12},{13,14},{15,16},{17,18},{19... | collective-permute-start | bytes 983048 | tf_op jit(solution)/shard_map/ppermute | solution.py:258
  4.1 9.1 %collective-permute-start = (f32[5,8,2048]{2,1,0:T(8,128)S(1)}, f32[5,8,2048]{2,1,0:T(8,128)S(1)}, u32[]{:S(2)}, u32[]{:S(2)}) collective-permute-start(f32[5,8,2048]{2,1,0:T(8,128)S(1)} %get-tuple-element.7.after_ref.own_near_ref), channel_id=1, source_target_pairs={{0,1},{1,0},{2,3},{3,2},{4,5},{5,4},{6,7},{7,6},{8,9},{9,8},{10,11... | collective-permute-start | bytes 983048 | tf_op jit(solution)/shard_map/ppermute | solution.py:259

commit v3 on v2

--- a/solution.py
+++ b/solution.py
@@ -26,18 +26,26 @@
     return pltpu.CompilerParams(vmem_limit_bytes=GRANT)
 
 
+def row_of(line, parity):
+    return line if parity == 0 else 2 * STEPS - 1 - line
+
+
 def pack_kernel(strip_ref, ens_ref, forcing_ref, cross_ref, near_ref):
     odd = lax.rem(strip_ref[0], 2)
-    for parity, low, high in ((0, cross_ref, near_ref), (1, near_ref, cross_ref)):
+    half = cross_ref.shape[2]
+    for parity in (0, 1):
 
         @pl.when(odd == parity)
         def _():
-            for row in range(STEPS):
-                low[row] = ens_ref[:, row, :]
-                high[row] = ens_ref[:, STEPS + row, :]
-
-    cross_ref[STEPS] = forcing_ref[...]
-    near_ref[STEPS] = forcing_ref[...]
+            for line in range(2 * STEPS):
+                message = cross_ref if line < STEPS else near_ref
+                at, row = line % STEPS, row_of(line, parity)
+                state, force = ens_ref[:, row, :], forcing_ref[row : row + 1, :]
+                for side in range(2):
+                    lons = slice(side * half, (side + 1) * half)
+                    message[2 * at + side] = state[:, lons]
+                    spot = side * STEPS + at
+                    message[2 * STEPS, spot : spot + 1, :] = force[:, lons]
 
 
 def columns_kernel(count_ref, index_ref, value_ref, precision_ref, after_ref, columns_ref):
@@ -56,54 +64,93 @@
     columns_ref[...] = jnp.concatenate(lines, axis=0).T
 
 
-def forecast_kernel(last, strip_ref, after_ref, own_near_ref, own_cross_ref, got_near_ref, got_cross_ref, out_ref, even_ref, other_ref, forcing_ref):
+def state_of(message, at):
+    return jnp.concatenate([message[2 * at], message[2 * at + 1]], axis=1)
+
+
+def force_of(message, at):
+    both = [message[2 * STEPS, spot : spot + 1, :] for spot in (at, STEPS + at)]
+    return jnp.concatenate(both, axis=1)
+
+
+def advance(before, center, after, force):
+    lon = center.shape[1]
+    west = pltpu.roll(center, 1, 1)
+    west2 = pltpu.roll(center, 2, 1)
+    east = pltpu.roll(center, lon - 1, 1)
+    return (
+        center * (1.0 - step_size - 2.0 * coupling)
+        + step_size * ((east - west2) * west + force)
+        + coupling * (before + after)
+    )
+
+
+def put_line(out_ref, odd, line, value):
+    width = out_ref.shape[2]
+    parts = value.shape[1] // width
+    for parity in (0, 1):
+
+        @pl.when(odd == parity)
+        def _():
+            for part in range(parts):
+                chunk = row_of(line, parity) * parts + part
+                out_ref[chunk] = value[:, part * width : (part + 1) * width]
+
+
+def near_kernel(after_ref, own_cross_ref, own_near_ref, got_near_ref, done_ref, edge_ref, *levels):
+    def start(read):
+        def of(line):
+            if line < STEPS:
+                return read(own_cross_ref, line)
+            if line < 2 * STEPS:
+                return read(own_near_ref, line - STEPS)
+            return read(got_near_ref, 3 * STEPS - 1 - line)
+
+        return of
+
+    force = start(force_of)
+    read = start(state_of)
+    for step in range(1, STEPS + 1):
+        for line in range(step, 3 * STEPS - step):
+            new = advance(read(line - 1), read(line), read(line + 1), force(line))
+            if step == STEPS:
+                done_ref[line - STEPS] = new
+            else:
+                levels[step - 1][line - step] = new
+                if line < step + 2:
+                    edge_ref[2 * (step - 1) + line - step] = new
+        if step < STEPS:
+            read = lambda line, step=step: levels[step - 1][line - step]
+
+
+def cross_kernel(last, strip_ref, done_ref, own_cross_ref, got_cross_ref, edge_ref, out_ref, *levels):
     strip = strip_ref[0]
     odd = lax.rem(strip, 2)
-    rows = 2 * STEPS
-    lon = out_ref.shape[0] * out_ref.shape[2] // rows
-    own_cross_at = STEPS + STEPS * odd
-    own_near_at = 2 * STEPS - STEPS * odd
-    got_cross_at = 3 * STEPS * odd
-    got_near_at = 3 * STEPS - 3 * STEPS * odd
-    for row in range(STEPS):
-        even_ref[own_cross_at + row] = own_cross_ref[row]
-        even_ref[own_near_at + row] = own_near_ref[row]
-        even_ref[got_cross_at + row] = got_cross_ref[row]
-        even_ref[got_near_at + row] = got_near_ref[row]
-    forcing_ref[1] = own_near_ref[STEPS]
-    forcing_ref[2 * odd] = got_cross_ref[STEPS]
-    forcing_ref[2 - 2 * odd] = got_near_ref[STEPS]
-    low_kept = jnp.where(strip == 0, 0.0, 1.0)
-    high_kept = jnp.where(strip == last, 0.0, 1.0)
-    buffers = (even_ref, other_ref)
-    for step in range(STEPS):
-        source, target = buffers[step % 2], buffers[(step + 1) % 2]
-        final = step == STEPS - 1
-
-        for row in range(step + 1, rows + 2 * STEPS - 1 - step):
-            center = source[row]
-            around = source[row - 1] + source[row + 1]
-            far = row + rows - STEPS
-            force = forcing_ref[far // rows, far % rows : far % rows + 1, :]
-            west = pltpu.roll(center, 1, 1)
-            west2 = pltpu.roll(center, 2, 1)
-            east = pltpu.roll(center, lon - 1, 1)
-            new = (
-                center * (1.0 - step_size - 2.0 * coupling)
-                + step_size * ((east - west2) * west + force)
-                + coupling * around
-            )
-            if final:
-                width = out_ref.shape[2]
-                parts = lon // width
-                for part in range(parts):
-                    out_ref[(row - STEPS) * parts + part] = new[:, part * width : (part + 1) * width]
-            elif row < STEPS:
-                target[row] = new * low_kept
-            elif row >= STEPS + rows:
-                target[row] = new * high_kept
+    kept = jnp.where(jnp.logical_or(strip == 0, strip == last), 0.0, 1.0)
+
+    def start(read):
+        return lambda line: read(own_cross_ref, line) if line >= 0 else read(got_cross_ref, -1 - line)
+
+    for line in range(STEPS):
+        put_line(out_ref, odd, STEPS + line, done_ref[line])
+    force = start(force_of)
+    read = start(state_of)
+    for step in range(1, STEPS + 1):
+        first = step - STEPS
+        for line in range(first, first + STEPS):
+            new = advance(read(line - 1), read(line), read(line + 1), force(line))
+            if line < 0:
+                new = new * kept
+            if step == STEPS:
+                put_line(out_ref, odd, line, new)
             else:
-                target[row] = new
+                levels[step - 1][line - first] = new
+        if step < STEPS:
+
+            def read(line, step=step, first=first):
+                if line < step:
+                    return levels[step - 1][line - first]
+                return edge_ref[2 * (step - 1) + line - step]
 
 
 NN = (((1,), (0,)), ((), ()))
@@ -242,11 +289,11 @@
     strips = lax.axis_size("strip")
     strip = lax.axis_index("strip").astype(jnp.int32).reshape(1)
     regions, slots = obs_index.shape
-    slab = jax.ShapeDtypeStruct((STEPS + 1, per, lon), jnp.float32)
+    message = jax.ShapeDtypeStruct((2 * STEPS + 1, per, lon // 2), jnp.float32)
 
     cross, near = pl.pallas_call(
         pack_kernel,
-        out_shape=(slab, slab),
+        out_shape=(message, message),
         in_specs=[SMEM, VMEM, VMEM],
         out_specs=(VMEM, VMEM),
         compiler_params=params(),
@@ -268,19 +315,30 @@
     )(obs_count, obs_index, obs_value, obs_precision, near)
     chunks = lax.axis_size("mem")
     width = rows * lon // chunks
+    full = jax.ShapeDtypeStruct((chunks, per, width), jnp.float32)
+
+    def line_slabs(count):
+        return pltpu.VMEM((count, per, lon), jnp.float32)
+
+    done, edges = pl.pallas_call(
+        near_kernel,
+        out_shape=tuple(jax.ShapeDtypeStruct((count, per, lon), jnp.float32) for count in (STEPS, 2 * (STEPS - 1))),
+        in_specs=[ANY] + [VMEM] * 3,
+        out_specs=(VMEM, VMEM),
+        scratch_shapes=[line_slabs(3 * STEPS - 2 * step) for step in range(1, STEPS)],
+        compiler_params=params(),
+        cost_estimate=pl.CostEstimate(flops=10**8, bytes_accessed=4096, transcendentals=0),
+        name="forecast_near",
+    )(columns, cross, near, got_near)
     sent = pl.pallas_call(
-        functools.partial(forecast_kernel, strips - 1),
-        out_shape=jax.ShapeDtypeStruct((chunks, per, width), jnp.float32),
-        in_specs=[SMEM, ANY] + [VMEM] * 4,
+        functools.partial(cross_kernel, strips - 1),
+        out_shape=full,
+        in_specs=[SMEM] + [VMEM] * 4,
         out_specs=VMEM,
-        scratch_shapes=[
-            pltpu.VMEM((4 * STEPS, per, lon), jnp.float32),
-            pltpu.VMEM((4 * STEPS, per, lon), jnp.float32),
-            pltpu.VMEM((3, rows, lon), jnp.float32),
-        ],
-        compiler_params=params(),
-        name="forecast",
-    )(strip, columns, near, cross, got_near, got_cross)
+        scratch_shapes=[line_slabs(STEPS) for _ in range(1, STEPS)],
+        compiler_params=params(),
+        name="forecast_cross",
+    )(strip, done, cross, got_cross, edges)
     regional = lax.all_to_all(sent, "mem", split_axis=0, concat_axis=0, tiled=True)
     analysed = pl.pallas_call(
         analysis_kernel,

time: 78.3 us -> 78.1 us (level)
  waiting for transfers between devices: 4.2 us -> 6.26 us
  starting transfers between devices: 6.22 us -> 4.39 us
    ppermute x1, starting transfers between devices: 4.17 us -> 2.05 us  [local(): got_near = lax.ppermute(near, 'strip', swap)]
    ppermute x1, waiting for transfers between devices: 4.19 us -> 6.26 us  [local(): got_cross = lax.ppermute(cross, 'strip', span)]
    pallas_call x2 -> x3, Pallas kernels: 2.81 us -> 2.95 us  [the longest x1 1.63 us: local(): pl.pallas_call(near_kernel, out_shape=tuple((jax.ShapeDtypeStruct((count,...]
  transfers between devices with their start and end apart: 2 -> 2, of which waited for: 1 -> 1; matrix products, arithmetic and copies ran while one was open for 0% -> 0% of each run, Pallas kernels for 1% -> 3%
where the time goes in v3:
time: 78.1 us; the launch traced here: 77.8 us
  blocking collectives  57.9 us (74%)
  Pallas kernels  7.18 us (9%)
  waiting for transfers between devices  6.26 us (8%)
  starting transfers between devices  4.39 us (6%)
  local copies, waits for them, and re-layouts  1.91 us (2%)
    all_to_all x1, blocking collectives, local(): lax.all_to_all(sent, 'mem', split_axis=0, concat_axis=0, tiled=True)  32.9 us
    all_to_all x1, blocking collectives, local(): lax.all_to_all(analysed, 'mem', split_axis=0, concat_axis=0, tiled=True)  25 us
    ppermute x1, waiting for transfers between devices, local(): got_cross = lax.ppermute(cross, 'strip', span)  6.26 us
    pallas_call x1, Pallas kernels, local(): pl.pallas_call(analysis_kernel, out_shape=jax.ShapeDtypeStruct((chunks, p...  2.65 us
    ppermute x1, starting transfers between devices, local(): got_cross = lax.ppermute(cross, 'strip', span)  2.34 us
    ppermute x1, starting transfers between devices, local(): got_near = lax.ppermute(near, 'strip', swap)  2.05 us
    unnamed x12, local copies, waits for them, and re-layouts  1.91 us
    pallas_call x1, Pallas kernels, local(): pl.pallas_call(near_kernel, out_shape=tuple((jax.ShapeDtypeStruct((count,...  1.63 us
  transfers between devices with their start and end apart: 2, of which 1 were waited for; matrix products, arithmetic and copies ran while one was open for 0% of the time, Pallas kernels for 3%

profile of v3, /device:TPU:786, one launch (start us, length us, event | category | flops | bytes accessed | tf_op | source)
XLA Modules:
  0.0 77.8 jit_solution(10201931420101416203)
XLA Ops:
  0.0 0.0 copy-start
  0.0 1.0 %copy-done = f32[8,8,2048]{2,1,0:T(8,128)S(1)} copy-done((f32[8,8,2048]{2,1,0:T(8,128)S(1)}, f32[8,8,2048]{2,1,0:T(8,128)}, u32[]{:S(2)}) %copy-start) | copy-done | bytes 524312
  1.0 0.0 copy-start.1
  1.0 0.8 %copy-done.1 = f32[8,2048]{1,0:T(8,128)S(1)} copy-done((f32[8,2048]{1,0:T(8,128)S(1)}, f32[8,2048]{1,0:T(8,128)}, u32[]{:S(2)}) %copy-start.1) | copy-done | bytes 65560
  1.9 0.1 pack.1
  2.0 0.0 copy-start.3
  2.0 0.0 copy-start.4
  2.0 0.0 copy-start.2
  2.1 0.0 copy-start.5
  2.1 2.1 %collective-permute-start = (f32[9,8,1024]{2,1,0:T(8,128)S(1)}, f32[9,8,1024]{2,1,0:T(8,128)S(1)}, u32[]{:S(2)}, u32[]{:S(2)}) collective-permute-start(f32[9,8,1024]{2,1,0:T(8,128)S(1)} %get-tuple-element.9.after_ref.own_near_ref), channel_id=1, source_target_pairs={{0,1},{1,0},{2,3},{3,2},{4,5},{5,4},{6,7},{7,6},{8,9},{9,8},{10,11... | collective-permute-start | bytes 884744 | tf_op jit(solution)/shard_map/ppermute | solution.py:306
  4.1 2.3 %collective-permute-start.1 = (f32[9,8,1024]{2,1,0:T(8,128)S(1)}, f32[9,8,1024]{2,1,0:T(8,128)S(1)}, u32[]{:S(2)}, u32[]{:S(2)}) collective-permute-start(f32[9,8,1024]{2,1,0:T(8,128)S(1)} %get-tuple-element.10.own_cross_ref), channel_id=1, source_target_pairs={{1,2},{3,4},{5,6},{7,8},{9,10},{11,12},{13,14},{15,16},{17,18},{19... | collective-permute-start | bytes 884744 | tf_op jit(solution)/shard_map/ppermute | solution.py:305
  6.5 0.0 copy-done.3
  6.5 0.0 copy-done.4
  6.5 0.0 copy-done.2
  6.5 0.0 copy-done.5
  6.5 0.7 columns.1.after_ref.columns_ref
  7.2 0.0 collective-permute-done.got_near_ref
  7.2 1.6 %forecast_near.1 = (f32[4,8,2048]{2,1,0:T(8,128)S(1)}, f32[6,8,2048]{2,1,0:T(8,128)S(1)}) custom-call(f32[128,8]{1,0:T(8,128)S(1)} %columns.1.after_ref.columns_ref, f32[9,8,1024]{2,1,0:T(8,128)S(1)} %get-tuple-element.10.own_cross_ref, f32[9,8,1024]{2,1,0:T(8,128)S(1)} %get-tuple-element.9.after_ref.own_near_ref, ...), custom_call_target="tpu_custom_call" | custom-call | flops 100000000 | bytes 4096 | tf_op jit(solution)/shard_map/forecast_near/pallas_call | solution.py:323
  8.8 6.3 %collective-permute-done.1.got_cross_ref = f32[9,8,1024]{2,1,0:T(8,128)S(1)} collective-permute-done((f32[9,8,1024]{2,1,0:T(8,128)S(1)}, f32[9,8,1024]{2,1,0:T(8,128)S(1)}, u32[]{:S(2)}, u32[]{:S(2)}) %collective-permute-start.1) | collective-permute-done | bytes 294944 | tf_op jit(solution)/shard_map/ppermute | solution.py:305
  15.1 1.2 %forecast_cross.1 = f32[32,8,512]{2,1,0:T(8,128)S(1)} custom-call(s32[1]{0:T(128)} %bitcast.strip_ref, f32[4,8,2048]{2,1,0:T(8,128)S(1)} %get-tuple-element.11.done_ref, f32[9,8,1024]{2,1,0:T(8,128)S(1)} %get-tuple-element.10.own_cross_ref, f32[9,8,1024]{2,1,0:T(8,128)S(1)} %collective-permute-done.1.got_cross_ref, f32[6,8,2048]{2,1,0:T(8,128)S(1)} %get-tuple-element.12.edge_ref), custom_call_target="tpu_custom_call" | custom-call | tf_op jit(solution)/shard_map/forecast_cross/pallas_call | solution.py:333
  16.3 32.9 %all_to_all.10.block_ref = f32[32,8,512]{2,1,0:T(8,128)S(1)} all-to-all(f32[32,8,512]{2,1,0:T(8,128)S(1)} %forecast_cross.1), channel_id=1, replica_groups=mesh['mem'=32,'strip'=32] {'mem'}, dimensions={0} | all-to-all | bytes 1048576 | tf_op jit(solution)/shard_map/all_to_all | solution.py:342
  49.2 2.6 %analysis.1 = f32[32,8,512]{2,1,0:T(8,128)S(1)} custom-call(f32[128,8]{1,0:T(8,128)S(1)} %columns.1.after_ref.columns_ref, f32[32,8,512]{2,1,0:T(8,128)S(1)} %all_to_all.10.block_ref), custom_call_target="tpu_custom_call" | custom-call | tf_op jit(solution)/shard_map/analysis/pallas_call | solution.py:343
  51.8 25.0 %all_to_all.11.block_ref = f32[32,8,512]{2,1,0:T(8,128)S(1)} all-to-all(f32[32,8,512]{2,1,0:T(8,128)S(1)} %analysis.1), channel_id=1, replica_groups=mesh['mem'=32,'strip'=32] {'mem'}, dimensions={0} | all-to-all | bytes 1048576 | tf_op jit(solution)/shard_map/all_to_all | solution.py:351
  76.9 0.9 %unpack.1 = f32[8,8,2048]{2,1,0:T(8,128)} custom-call(f32[32,8,512]{2,1,0:T(8,128)S(1)} %all_to_all.11.block_ref), custom_call_target="tpu_custom_call" | custom-call | tf_op jit(solution)/shard_map/unpack/pallas_call | solution.py:352
Async XLA Ops:
  0.0 1.0 %copy-start = (f32[8,8,2048]{2,1,0:T(8,128)S(1)}, f32[8,8,2048]{2,1,0:T(8,128)}, u32[]{:S(2)}) copy-start(f32[8,8,2048]{2,1,0:T(8,128)} %ens_ref.1) | copy-start | bytes 1572868
  1.0 0.8 %copy-start.1 = (f32[8,2048]{1,0:T(8,128)S(1)}, f32[8,2048]{1,0:T(8,128)}, u32[]{:S(2)}) copy-start(f32[8,2048]{1,0:T(8,128)} %forcing_ref.1) | copy-start | bytes 196612
  2.0 4.5 %copy-start.3 = (f32[2,128]{1,0:T(2,128)S(1)}, f32[2,128]{1,0:T(2,128)}, u32[]{:S(2)}) copy-start(f32[2,128]{1,0:T(2,128)} %value_ref.1) | copy-start | bytes 3076
  2.0 4.5 %copy-start.4 = (f32[2,128]{1,0:T(2,128)S(1)}, f32[2,128]{1,0:T(2,128)}, u32[]{:S(2)}) copy-start(f32[2,128]{1,0:T(2,128)} %precision_ref.1) | copy-start | bytes 3076
  2.0 4.5 %copy-start.2 = (s32[2,128]{1,0:T(2,128)S(1)}, s32[2,128]{1,0:T(2,128)}, u32[]{:S(2)}) copy-start(s32[2,128]{1,0:T(2,128)} %index_ref.1) | copy-start | bytes 3076
  2.1 4.5 %copy-start.5 = (s32[2]{0:T(128)S(1)}, s32[2]{0:T(128)}, u32[]{:S(2)}) copy-start(s32[2]{0:T(128)} %count_ref.1) | copy-start | bytes 28
  2.1 5.1 %collective-permute-start = (f32[9,8,1024]{2,1,0:T(8,128)S(1)}, f32[9,8,1024]{2,1,0:T(8,128)S(1)}, u32[]{:S(2)}, u32[]{:S(2)}) collective-permute-start(f32[9,8,1024]{2,1,0:T(8,128)S(1)} %get-tuple-element.9.after_ref.own_near_ref), channel_id=1, source_target_pairs={{0,1},{1,0},{2,3},{3,2},{4,5},{5,4},{6,7},{7,6},{8,9},{9,8},{10,11... | collective-permute-start | bytes 884744 | tf_op jit(solution)/shard_map/ppermute | solution.py:306
  4.1 11.0 %collective-permute-start.1 = (f32[9,8,1024]{2,1,0:T(8,128)S(1)}, f32[9,8,1024]{2,1,0:T(8,128)S(1)}, u32[]{:S(2)}, u32[]{:S(2)}) collective-permute-start(f32[9,8,1024]{2,1,0:T(8,128)S(1)} %get-tuple-element.10.own_cross_ref), channel_id=1, source_target_pairs={{1,2},{3,4},{5,6},{7,8},{9,10},{11,12},{13,14},{15,16},{17,18},{19... | collective-permute-start | bytes 884744 | tf_op jit(solution)/shard_map/ppermute | solution.py:305

commit v4 on v3

--- a/solution.py
+++ b/solution.py
@@ -24,6 +24,13 @@
 
 def params():
     return pltpu.CompilerParams(vmem_limit_bytes=GRANT)
+
+
+LEAD = 20
+
+
+def rank_of(owner, count):
+    return (owner - LEAD) % count
 
 
 def row_of(line, parity):
@@ -93,7 +100,7 @@
         @pl.when(odd == parity)
         def _():
             for part in range(parts):
-                chunk = row_of(line, parity) * parts + part
+                chunk = rank_of(row_of(line, parity) * parts + part, out_ref.shape[0])
                 out_ref[chunk] = value[:, part * width : (part + 1) * width]
 
 
@@ -281,7 +288,7 @@
     width = block_ref.shape[2]
     for row in range(rows):
         for part in range(parts):
-            out_ref[:, row, part * width : (part + 1) * width] = block_ref[row * parts + part]
+            out_ref[:, row, part * width : (part + 1) * width] = block_ref[rank_of(row * parts + part, block_ref.shape[0])]
 
 
 def local(ensemble, forcing, obs_index, obs_count, obs_value, obs_precision):
@@ -339,7 +346,12 @@
         compiler_params=params(),
         name="forecast_cross",
     )(strip, done, cross, got_cross, edges)
-    regional = lax.all_to_all(sent, "mem", split_axis=0, concat_axis=0, tiled=True)
+    ranks = sorted(range(chunks), key=lambda owner: rank_of(owner, chunks))
+
+    def exchange(x):
+        return lax.all_to_all(x, "mem", split_axis=0, concat_axis=0, axis_index_groups=[ranks], tiled=True)
+
+    regional = exchange(sent)
     analysed = pl.pallas_call(
         analysis_kernel,
         out_shape=jax.ShapeDtypeStruct((chunks, per, width), jnp.float32),
@@ -348,7 +360,7 @@
         compiler_params=params(),
         name="analysis",
     )(columns, regional)
-    back = lax.all_to_all(analysed, "mem", split_axis=0, concat_axis=0, tiled=True)
+    back = exchange(analysed)
     return pl.pallas_call(
         unpack_kernel,
         out_shape=jax.ShapeDtypeStruct((per, rows, lon), jnp.float32),

time: 78.1 us -> 74.3 us (0.951)
  the two profiles are of different devices: /device:TPU:786 before, /device:TPU:1 now
where the time goes in v4:
time: 74.3 us; the launch traced here: 74 us
  blocking collectives  43 us (58%)
  starting transfers between devices  18.1 us (24%)
  Pallas kernels  7.18 us (10%)
  waiting for transfers between devices  3.77 us (5%)
  local copies, waits for them, and re-layouts  1.91 us (3%)
    all_to_all x2, blocking collectives, exchange(): lax.all_to_all(x, 'mem', split_axis=0, concat_axis=0, axis_index_groups=[...  43 us
    ppermute x1, starting transfers between devices, local(): got_near = lax.ppermute(near, 'strip', swap)  16.2 us
    ppermute x1, waiting for transfers between devices, local(): got_cross = lax.ppermute(cross, 'strip', span)  3.77 us
    pallas_call x1, Pallas kernels, local(): pl.pallas_call(analysis_kernel, out_shape=jax.ShapeDtypeStruct((chunks, p...  2.65 us
    ppermute x1, starting transfers between devices, local(): got_cross = lax.ppermute(cross, 'strip', span)  1.92 us
    unnamed x12, local copies, waits for them, and re-layouts  1.91 us
    pallas_call x1, Pallas kernels, local(): pl.pallas_call(near_kernel, out_shape=tuple((jax.ShapeDtypeStruct((count,...  1.63 us
  transfers between devices with their start and end apart: 2, of which 1 were waited for; matrix products, arithmetic and copies ran while one was open for 0% of the time, Pallas kernels for 3%

profile of v4, /device:TPU:1, one launch (start us, length us, event | category | flops | bytes accessed | tf_op | source)
XLA Modules:
  0.0 74.0 jit_solution(9351141788119760701)
XLA Ops:
  0.0 0.0 copy-start
  0.0 1.0 %copy-done = f32[8,8,2048]{2,1,0:T(8,128)S(1)} copy-done((f32[8,8,2048]{2,1,0:T(8,128)S(1)}, f32[8,8,2048]{2,1,0:T(8,128)}, u32[]{:S(2)}) %copy-start) | copy-done | bytes 524312
  1.0 0.0 copy-start.1
  1.0 0.8 %copy-done.1 = f32[8,2048]{1,0:T(8,128)S(1)} copy-done((f32[8,2048]{1,0:T(8,128)S(1)}, f32[8,2048]{1,0:T(8,128)}, u32[]{:S(2)}) %copy-start.1) | copy-done | bytes 65560
  1.9 0.1 pack.1
  2.0 0.0 copy-start.3
  2.0 0.0 copy-start.4
  2.0 0.0 copy-start.2
  2.1 0.0 copy-start.5
  2.1 16.2 %collective-permute-start = (f32[9,8,1024]{2,1,0:T(8,128)S(1)}, f32[9,8,1024]{2,1,0:T(8,128)S(1)}, u32[]{:S(2)}, u32[]{:S(2)}) collective-permute-start(f32[9,8,1024]{2,1,0:T(8,128)S(1)} %get-tuple-element.9.after_ref.own_near_ref), channel_id=1, source_target_pairs={{0,1},{1,0},{2,3},{3,2},{4,5},{5,4},{6,7},{7,6},{8,9},{9,8},{10,11... | collective-permute-start | bytes 884744 | tf_op jit(solution)/shard_map/ppermute | solution.py:313
  18.2 1.9 %collective-permute-start.1 = (f32[9,8,1024]{2,1,0:T(8,128)S(1)}, f32[9,8,1024]{2,1,0:T(8,128)S(1)}, u32[]{:S(2)}, u32[]{:S(2)}) collective-permute-start(f32[9,8,1024]{2,1,0:T(8,128)S(1)} %get-tuple-element.10.own_cross_ref), channel_id=1, source_target_pairs={{1,2},{3,4},{5,6},{7,8},{9,10},{11,12},{13,14},{15,16},{17,18},{19... | collective-permute-start | bytes 884744 | tf_op jit(solution)/shard_map/ppermute | solution.py:312
  20.2 0.0 copy-done.3
  20.2 0.0 copy-done.4
  20.2 0.0 copy-done.2
  20.2 0.0 copy-done.5
  20.2 0.7 columns.1.after_ref.columns_ref
  20.9 0.0 collective-permute-done.got_near_ref
  20.9 1.6 %forecast_near.1 = (f32[4,8,2048]{2,1,0:T(8,128)S(1)}, f32[6,8,2048]{2,1,0:T(8,128)S(1)}) custom-call(f32[128,8]{1,0:T(8,128)S(1)} %columns.1.after_ref.columns_ref, f32[9,8,1024]{2,1,0:T(8,128)S(1)} %get-tuple-element.10.own_cross_ref, f32[9,8,1024]{2,1,0:T(8,128)S(1)} %get-tuple-element.9.after_ref.own_near_ref, ...), custom_call_target="tpu_custom_call" | custom-call | flops 100000000 | bytes 4096 | tf_op jit(solution)/shard_map/forecast_near/pallas_call | solution.py:330
  22.5 3.8 %collective-permute-done.1.got_cross_ref = f32[9,8,1024]{2,1,0:T(8,128)S(1)} collective-permute-done((f32[9,8,1024]{2,1,0:T(8,128)S(1)}, f32[9,8,1024]{2,1,0:T(8,128)S(1)}, u32[]{:S(2)}, u32[]{:S(2)}) %collective-permute-start.1) | collective-permute-done | bytes 294944 | tf_op jit(solution)/shard_map/ppermute | solution.py:312
  26.3 1.2 %forecast_cross.1 = f32[32,8,512]{2,1,0:T(8,128)S(1)} custom-call(s32[1]{0:T(128)} %bitcast.strip_ref, f32[4,8,2048]{2,1,0:T(8,128)S(1)} %get-tuple-element.11.done_ref, f32[9,8,1024]{2,1,0:T(8,128)S(1)} %get-tuple-element.10.own_cross_ref, f32[9,8,1024]{2,1,0:T(8,128)S(1)} %collective-permute-done.1.got_cross_ref, f32[6,8,2048]{2,1,0:T(8,128)S(1)} %get-tuple-element.12.edge_ref), custom_call_target="tpu_custom_call" | custom-call | tf_op jit(solution)/shard_map/forecast_cross/pallas_call | solution.py:340
  27.5 19.8 %all_to_all.10.block_ref = f32[32,8,512]{2,1,0:T(8,128)S(1)} all-to-all(f32[32,8,512]{2,1,0:T(8,128)S(1)} %forecast_cross.1), channel_id=1, replica_groups={{640,672,704,736,768,800,832,864,896,928,960,992,0,32,64,96,128,160,192..., dimensions={0} | all-to-all | bytes 1048576 | tf_op jit(solution)/shard_map/all_to_all | solution.py:352
  47.3 2.6 %analysis.1 = f32[32,8,512]{2,1,0:T(8,128)S(1)} custom-call(f32[128,8]{1,0:T(8,128)S(1)} %columns.1.after_ref.columns_ref, f32[32,8,512]{2,1,0:T(8,128)S(1)} %all_to_all.10.block_ref), custom_call_target="tpu_custom_call" | custom-call | tf_op jit(solution)/shard_map/analysis/pallas_call | solution.py:355
  49.9 23.1 %all_to_all.11.block_ref = f32[32,8,512]{2,1,0:T(8,128)S(1)} all-to-all(f32[32,8,512]{2,1,0:T(8,128)S(1)} %analysis.1), channel_id=1, replica_groups={{640,672,704,736,768,800,832,864,896,928,960,992,0,32,64,96,128,160,192..., dimensions={0} | all-to-all | bytes 1048576 | tf_op jit(solution)/shard_map/all_to_all | solution.py:352
  73.1 0.9 %unpack.1 = f32[8,8,2048]{2,1,0:T(8,128)} custom-call(f32[32,8,512]{2,1,0:T(8,128)S(1)} %all_to_all.11.block_ref), custom_call_target="tpu_custom_call" | custom-call | tf_op jit(solution)/shard_map/unpack/pallas_call | solution.py:364
Async XLA Ops:
  0.0 1.0 %copy-start = (f32[8,8,2048]{2,1,0:T(8,128)S(1)}, f32[8,8,2048]{2,1,0:T(8,128)}, u32[]{:S(2)}) copy-start(f32[8,8,2048]{2,1,0:T(8,128)} %ens_ref.1) | copy-start | bytes 1572868
  1.0 0.8 %copy-start.1 = (f32[8,2048]{1,0:T(8,128)S(1)}, f32[8,2048]{1,0:T(8,128)}, u32[]{:S(2)}) copy-start(f32[8,2048]{1,0:T(8,128)} %forcing_ref.1) | copy-start | bytes 196612
  2.0 18.1 %copy-start.3 = (f32[2,128]{1,0:T(2,128)S(1)}, f32[2,128]{1,0:T(2,128)}, u32[]{:S(2)}) copy-start(f32[2,128]{1,0:T(2,128)} %value_ref.1) | copy-start | bytes 3076
  2.0 18.1 %copy-start.4 = (f32[2,128]{1,0:T(2,128)S(1)}, f32[2,128]{1,0:T(2,128)}, u32[]{:S(2)}) copy-start(f32[2,128]{1,0:T(2,128)} %precision_ref.1) | copy-start | bytes 3076
  2.0 18.1 %copy-start.2 = (s32[2,128]{1,0:T(2,128)S(1)}, s32[2,128]{1,0:T(2,128)}, u32[]{:S(2)}) copy-start(s32[2,128]{1,0:T(2,128)} %index_ref.1) | copy-start | bytes 3076
  2.1 18.1 %copy-start.5 = (s32[2]{0:T(128)S(1)}, s32[2]{0:T(128)}, u32[]{:S(2)}) copy-start(s32[2]{0:T(128)} %count_ref.1) | copy-start | bytes 28
  2.1 18.8 %collective-permute-start = (f32[9,8,1024]{2,1,0:T(8,128)S(1)}, f32[9,8,1024]{2,1,0:T(8,128)S(1)}, u32[]{:S(2)}, u32[]{:S(2)}) collective-permute-start(f32[9,8,1024]{2,1,0:T(8,128)S(1)} %get-tuple-element.9.after_ref.own_near_ref), channel_id=1, source_target_pairs={{0,1},{1,0},{2,3},{3,2},{4,5},{5,4},{6,7},{7,6},{8,9},{9,8},{10,11... | collective-permute-start | bytes 884744 | tf_op jit(solution)/shard_map/ppermute | solution.py:313
  18.2 8.0 %collective-permute-start.1 = (f32[9,8,1024]{2,1,0:T(8,128)S(1)}, f32[9,8,1024]{2,1,0:T(8,128)S(1)}, u32[]{:S(2)}, u32[]{:S(2)}) collective-permute-start(f32[9,8,1024]{2,1,0:T(8,128)S(1)} %get-tuple-element.10.own_cross_ref), channel_id=1, source_target_pairs={{1,2},{3,4},{5,6},{7,8},{9,10},{11,12},{13,14},{15,16},{17,18},{19... | collective-permute-start | bytes 884744 | tf_op jit(solution)/shard_map/ppermute | solution.py:312

commit v5 on v4

--- a/solution.py
+++ b/solution.py
@@ -26,11 +26,12 @@
     return pltpu.CompilerParams(vmem_limit_bytes=GRANT)
 
 
-LEAD = 20
-
-
-def rank_of(owner, count):
-    return (owner - LEAD) % count
+def leader_of(strip):
+    return jnp.where(strip < 2, 0, 20) if not isinstance(strip, int) else 0 if strip < 2 else 20
+
+
+def rank_of(owner, leader, count):
+    return lax.rem(owner + count - leader, count)
 
 
 def row_of(line, parity):
@@ -92,16 +93,13 @@
     )
 
 
-def put_line(out_ref, odd, line, value):
+def put_line(out_ref, odd, leader, line, value):
     width = out_ref.shape[2]
     parts = value.shape[1] // width
-    for parity in (0, 1):
-
-        @pl.when(odd == parity)
-        def _():
-            for part in range(parts):
-                chunk = rank_of(row_of(line, parity) * parts + part, out_ref.shape[0])
-                out_ref[chunk] = value[:, part * width : (part + 1) * width]
+    row = line + odd * (2 * STEPS - 1 - 2 * line)
+    for part in range(parts):
+        chunk = rank_of(row * parts + part, leader, out_ref.shape[0])
+        out_ref[chunk] = value[:, part * width : (part + 1) * width]
 
 
 def near_kernel(after_ref, own_cross_ref, own_near_ref, got_near_ref, done_ref, edge_ref, *levels):
@@ -133,13 +131,14 @@
 def cross_kernel(last, strip_ref, done_ref, own_cross_ref, got_cross_ref, edge_ref, out_ref, *levels):
     strip = strip_ref[0]
     odd = lax.rem(strip, 2)
+    leader = leader_of(strip)
     kept = jnp.where(jnp.logical_or(strip == 0, strip == last), 0.0, 1.0)
 
     def start(read):
         return lambda line: read(own_cross_ref, line) if line >= 0 else read(got_cross_ref, -1 - line)
 
     for line in range(STEPS):
-        put_line(out_ref, odd, STEPS + line, done_ref[line])
+        put_line(out_ref, odd, leader, STEPS + line, done_ref[line])
     force = start(force_of)
     read = start(state_of)
     for step in range(1, STEPS + 1):
@@ -149,7 +148,7 @@
             if line < 0:
                 new = new * kept
             if step == STEPS:
-                put_line(out_ref, odd, line, new)
+                put_line(out_ref, odd, leader, line, new)
             else:
                 levels[step - 1][line - first] = new
         if step < STEPS:
@@ -282,13 +281,14 @@
         finish(r, states[r])
 
 
-def unpack_kernel(block_ref, out_ref):
+def unpack_kernel(strip_ref, block_ref, out_ref):
+    leader = leader_of(strip_ref[0])
     rows = out_ref.shape[1]
     parts = block_ref.shape[0] // rows
     width = block_ref.shape[2]
     for row in range(rows):
         for part in range(parts):
-            out_ref[:, row, part * width : (part + 1) * width] = block_ref[rank_of(row * parts + part, block_ref.shape[0])]
+            out_ref[:, row, part * width : (part + 1) * width] = block_ref[rank_of(row * parts + part, leader, block_ref.shape[0])]
 
 
 def local(ensemble, forcing, obs_index, obs_count, obs_value, obs_precision):
@@ -346,10 +346,12 @@
         compiler_params=params(),
         name="forecast_cross",
     )(strip, done, cross, got_cross, edges)
-    ranks = sorted(range(chunks), key=lambda owner: rank_of(owner, chunks))
+    groups = [
+        [i * chunks + (leader_of(i) + rank) % chunks for rank in range(chunks)] for i in range(strips)
+    ]
 
     def exchange(x):
-        return lax.all_to_all(x, "mem", split_axis=0, concat_axis=0, axis_index_groups=[ranks], tiled=True)
+        return lax.all_to_all(x, ("strip", "mem"), split_axis=0, concat_axis=0, axis_index_groups=groups, tiled=True)
 
     regional = exchange(sent)
     analysed = pl.pallas_call(
@@ -364,11 +366,11 @@
     return pl.pallas_call(
         unpack_kernel,
         out_shape=jax.ShapeDtypeStruct((per, rows, lon), jnp.float32),
-        in_specs=[VMEM],
+        in_specs=[SMEM, VMEM],
         out_specs=VMEM,
         compiler_params=params(),
         name="unpack",
-    )(back)
+    )(strip, back)
 
 
 def solution(mesh):

time: 74.3 us -> 72.1 us (0.970)
  the two profiles are of different devices: /device:TPU:1 before, /device:TPU:3 now
where the time goes in v5:
time: 72.1 us; the launch traced here: 71.7 us
  blocking collectives  53.3 us (74%)
  Pallas kernels  6.94 us (10%)
  starting transfers between devices  5.94 us (8%)
  waiting for transfers between devices  3.59 us (5%)
  local copies, waits for them, and re-layouts  1.91 us (3%)
    all_to_all x2, blocking collectives, exchange(): lax.all_to_all(x, ('strip', 'mem'), split_axis=0, concat_axis=0, axis_ind...  53.3 us
    ppermute x1, waiting for transfers between devices, local(): got_cross = lax.ppermute(cross, 'strip', span)  3.58 us
    ppermute x1, starting transfers between devices, local(): got_cross = lax.ppermute(cross, 'strip', span)  3.22 us
    ppermute x1, starting transfers between devices, local(): got_near = lax.ppermute(near, 'strip', swap)  2.72 us
    pallas_call x1, Pallas kernels, local(): pl.pallas_call(analysis_kernel, out_shape=jax.ShapeDtypeStruct((chunks, p...  2.65 us
    unnamed x12, local copies, waits for them, and re-layouts  1.91 us
    pallas_call x1, Pallas kernels, local(): pl.pallas_call(near_kernel, out_shape=tuple((jax.ShapeDtypeStruct((count,...  1.63 us
  transfers between devices with their start and end apart: 2, of which 1 were waited for; matrix products, arithmetic and copies ran while one was open for 0% of the time, Pallas kernels for 3%

profile of v5, /device:TPU:3, one launch (start us, length us, event | category | flops | bytes accessed | tf_op | source)
XLA Modules:
  0.0 71.7 jit_solution(979754683135105553)
XLA Ops:
  0.0 0.0 copy-start
  0.0 1.0 %copy-done = f32[8,8,2048]{2,1,0:T(8,128)S(1)} copy-done((f32[8,8,2048]{2,1,0:T(8,128)S(1)}, f32[8,8,2048]{2,1,0:T(8,128)}, u32[]{:S(2)}) %copy-start) | copy-done | bytes 524312
  1.0 0.0 copy-start.1
  1.0 0.8 %copy-done.1 = f32[8,2048]{1,0:T(8,128)S(1)} copy-done((f32[8,2048]{1,0:T(8,128)S(1)}, f32[8,2048]{1,0:T(8,128)}, u32[]{:S(2)}) %copy-start.1) | copy-done | bytes 65560
  1.9 0.1 pack.1
  2.0 0.0 copy-start.3
  2.0 0.0 copy-start.4
  2.0 0.0 copy-start.2
  2.1 0.0 copy-start.5
  2.1 2.7 %collective-permute-start = (f32[9,8,1024]{2,1,0:T(8,128)S(1)}, f32[9,8,1024]{2,1,0:T(8,128)S(1)}, u32[]{:S(2)}, u32[]{:S(2)}) collective-permute-start(f32[9,8,1024]{2,1,0:T(8,128)S(1)} %get-tuple-element.9.after_ref.own_near_ref), channel_id=1, source_target_pairs={{0,1},{1,0},{2,3},{3,2},{4,5},{5,4},{6,7},{7,6},{8,9},{9,8},{10,11... | collective-permute-start | bytes 884744 | tf_op jit(solution)/shard_map/ppermute | solution.py:313
  4.8 3.2 %collective-permute-start.1 = (f32[9,8,1024]{2,1,0:T(8,128)S(1)}, f32[9,8,1024]{2,1,0:T(8,128)S(1)}, u32[]{:S(2)}, u32[]{:S(2)}) collective-permute-start(f32[9,8,1024]{2,1,0:T(8,128)S(1)} %get-tuple-element.10.own_cross_ref), channel_id=1, source_target_pairs={{1,2},{3,4},{5,6},{7,8},{9,10},{11,12},{13,14},{15,16},{17,18},{19... | collective-permute-start | bytes 884744 | tf_op jit(solution)/shard_map/ppermute | solution.py:312
  8.0 0.0 copy-done.3
  8.0 0.0 copy-done.4
  8.0 0.0 copy-done.2
  8.0 0.0 copy-done.5
  8.1 0.7 columns.1.after_ref.columns_ref
  8.7 0.0 collective-permute-done.got_near_ref
  8.7 1.6 %forecast_near.1 = (f32[4,8,2048]{2,1,0:T(8,128)S(1)}, f32[6,8,2048]{2,1,0:T(8,128)S(1)}) custom-call(f32[128,8]{1,0:T(8,128)S(1)} %columns.1.after_ref.columns_ref, f32[9,8,1024]{2,1,0:T(8,128)S(1)} %get-tuple-element.10.own_cross_ref, f32[9,8,1024]{2,1,0:T(8,128)S(1)} %get-tuple-element.9.after_ref.own_near_ref, ...), custom_call_target="tpu_custom_call" | custom-call | flops 100000000 | bytes 4096 | tf_op jit(solution)/shard_map/forecast_near/pallas_call | solution.py:330
  10.4 3.6 %collective-permute-done.1.got_cross_ref = f32[9,8,1024]{2,1,0:T(8,128)S(1)} collective-permute-done((f32[9,8,1024]{2,1,0:T(8,128)S(1)}, f32[9,8,1024]{2,1,0:T(8,128)S(1)}, u32[]{:S(2)}, u32[]{:S(2)}) %collective-permute-start.1) | collective-permute-done | bytes 294944 | tf_op jit(solution)/shard_map/ppermute | solution.py:312
  13.9 0.9 %forecast_cross.1 = f32[32,8,512]{2,1,0:T(8,128)S(1)} custom-call(s32[1]{0:T(128)} %bitcast.strip_ref, f32[4,8,2048]{2,1,0:T(8,128)S(1)} %get-tuple-element.11.done_ref, f32[9,8,1024]{2,1,0:T(8,128)S(1)} %get-tuple-element.10.own_cross_ref, f32[9,8,1024]{2,1,0:T(8,128)S(1)} %collective-permute-done.1.got_cross_ref, f32[6,8,2048]{2,1,0:T(8,128)S(1)} %get-tuple-element.12.edge_ref), custom_call_target="tpu_custom_call" | custom-call | tf_op jit(solution)/shard_map/forecast_cross/pallas_call | solution.py:340
  14.9 31.1 %all_to_all.10.block_ref = f32[32,8,512]{2,1,0:T(8,128)S(1)} all-to-all(f32[32,8,512]{2,1,0:T(8,128)S(1)} %forecast_cross.1), channel_id=1, replica_groups={{0,32,64,96,128,160,192,224,256,288,320,352,384,416,448,480,512,544,576..., dimensions={0} | all-to-all | bytes 1048576 | tf_op jit(solution)/shard_map/all_to_all | solution.py:354
  46.0 2.6 %analysis.1 = f32[32,8,512]{2,1,0:T(8,128)S(1)} custom-call(f32[128,8]{1,0:T(8,128)S(1)} %columns.1.after_ref.columns_ref, f32[32,8,512]{2,1,0:T(8,128)S(1)} %all_to_all.10.block_ref), custom_call_target="tpu_custom_call" | custom-call | tf_op jit(solution)/shard_map/analysis/pallas_call | solution.py:357
  48.7 22.1 %all_to_all.11.block_ref = f32[32,8,512]{2,1,0:T(8,128)S(1)} all-to-all(f32[32,8,512]{2,1,0:T(8,128)S(1)} %analysis.1), channel_id=1, replica_groups={{0,32,64,96,128,160,192,224,256,288,320,352,384,416,448,480,512,544,576..., dimensions={0} | all-to-all | bytes 1048576 | tf_op jit(solution)/shard_map/all_to_all | solution.py:354
  70.8 0.9 %unpack.1 = f32[8,8,2048]{2,1,0:T(8,128)} custom-call(s32[1]{0:T(128)} %bitcast.strip_ref, f32[32,8,512]{2,1,0:T(8,128)S(1)} %all_to_all.11.block_ref), custom_call_target="tpu_custom_call" | custom-call | tf_op jit(solution)/shard_map/unpack/pallas_call | solution.py:366
Async XLA Ops:
  0.0 1.0 %copy-start = (f32[8,8,2048]{2,1,0:T(8,128)S(1)}, f32[8,8,2048]{2,1,0:T(8,128)}, u32[]{:S(2)}) copy-start(f32[8,8,2048]{2,1,0:T(8,128)} %ens_ref.1) | copy-start | bytes 1572868
  1.0 0.8 %copy-start.1 = (f32[8,2048]{1,0:T(8,128)S(1)}, f32[8,2048]{1,0:T(8,128)}, u32[]{:S(2)}) copy-start(f32[8,2048]{1,0:T(8,128)} %forcing_ref.1) | copy-start | bytes 196612
  2.0 6.0 %copy-start.3 = (f32[2,128]{1,0:T(2,128)S(1)}, f32[2,128]{1,0:T(2,128)}, u32[]{:S(2)}) copy-start(f32[2,128]{1,0:T(2,128)} %value_ref.1) | copy-start | bytes 3076
  2.0 6.0 %copy-start.4 = (f32[2,128]{1,0:T(2,128)S(1)}, f32[2,128]{1,0:T(2,128)}, u32[]{:S(2)}) copy-start(f32[2,128]{1,0:T(2,128)} %precision_ref.1) | copy-start | bytes 3076
  2.0 6.0 %copy-start.2 = (s32[2,128]{1,0:T(2,128)S(1)}, s32[2,128]{1,0:T(2,128)}, u32[]{:S(2)}) copy-start(s32[2,128]{1,0:T(2,128)} %index_ref.1) | copy-start | bytes 3076
  2.1 6.0 %copy-start.5 = (s32[2]{0:T(128)S(1)}, s32[2]{0:T(128)}, u32[]{:S(2)}) copy-start(s32[2]{0:T(128)} %count_ref.1) | copy-start | bytes 28
  2.1 6.7 %collective-permute-start = (f32[9,8,1024]{2,1,0:T(8,128)S(1)}, f32[9,8,1024]{2,1,0:T(8,128)S(1)}, u32[]{:S(2)}, u32[]{:S(2)}) collective-permute-start(f32[9,8,1024]{2,1,0:T(8,128)S(1)} %get-tuple-element.9.after_ref.own_near_ref), channel_id=1, source_target_pairs={{0,1},{1,0},{2,3},{3,2},{4,5},{5,4},{6,7},{7,6},{8,9},{9,8},{10,11... | collective-permute-start | bytes 884744 | tf_op jit(solution)/shard_map/ppermute | solution.py:313
  4.8 9.2 %collective-permute-start.1 = (f32[9,8,1024]{2,1,0:T(8,128)S(1)}, f32[9,8,1024]{2,1,0:T(8,128)S(1)}, u32[]{:S(2)}, u32[]{:S(2)}) collective-permute-start(f32[9,8,1024]{2,1,0:T(8,128)S(1)} %get-tuple-element.10.own_cross_ref), channel_id=1, source_target_pairs={{1,2},{3,4},{5,6},{7,8},{9,10},{11,12},{13,14},{15,16},{17,18},{19... | collective-permute-start | bytes 884744 | tf_op jit(solution)/shard_map/ppermute | solution.py:312

commit v6 on v5

--- a/solution.py
+++ b/solution.py
@@ -46,8 +46,9 @@
         @pl.when(odd == parity)
         def _():
             for line in range(2 * STEPS):
-                message = cross_ref if line < STEPS else near_ref
-                at, row = line % STEPS, row_of(line, parity)
+                inner = line < STEPS
+                message, at = (cross_ref, line) if inner else (near_ref, 2 * STEPS - 1 - line)
+                row = row_of(line, parity)
                 state, force = ens_ref[:, row, :], forcing_ref[row : row + 1, :]
                 for side in range(2):
                     lons = slice(side * half, (side + 1) * half)
@@ -56,7 +57,40 @@
                     message[2 * STEPS, spot : spot + 1, :] = force[:, lons]
 
 
-def columns_kernel(count_ref, index_ref, value_ref, precision_ref, after_ref, columns_ref):
+def state_of(message, at):
+    return jnp.concatenate([message[2 * at], message[2 * at + 1]], axis=1)
+
+
+def force_of(message, at):
+    both = [message[2 * STEPS, spot : spot + 1, :] for spot in (at, STEPS + at)]
+    return jnp.concatenate(both, axis=1)
+
+
+def advance(before, center, after, force):
+    lon = center.shape[1]
+    west = pltpu.roll(center, 1, 1)
+    west2 = pltpu.roll(center, 2, 1)
+    east = pltpu.roll(center, lon - 1, 1)
+    return (
+        center * (1.0 - step_size - 2.0 * coupling)
+        + step_size * ((east - west2) * west + force)
+        + coupling * (before + after)
+    )
+
+
+def put_line(out_ref, odd, leader, line, value):
+    width = out_ref.shape[2]
+    parts = value.shape[1] // width
+    row = line + odd * (2 * STEPS - 1 - 2 * line)
+    for part in range(parts):
+        chunk = rank_of(row * parts + part, leader, out_ref.shape[0])
+        out_ref[chunk] = value[:, part * width : (part + 1) * width]
+
+
+def own_kernel(
+    count_ref, index_ref, value_ref, precision_ref, own_cross_ref, own_near_ref,
+    columns_ref, cross_edge_ref, near_edge_ref, *levels
+):
     slots = index_ref.shape[1]
     slot = lax.broadcasted_iota(jnp.int32, (1, slots), 1)
     lines = []
@@ -71,92 +105,62 @@
         ]
     columns_ref[...] = jnp.concatenate(lines, axis=0).T
 
-
-def state_of(message, at):
-    return jnp.concatenate([message[2 * at], message[2 * at + 1]], axis=1)
-
-
-def force_of(message, at):
-    both = [message[2 * STEPS, spot : spot + 1, :] for spot in (at, STEPS + at)]
-    return jnp.concatenate(both, axis=1)
-
-
-def advance(before, center, after, force):
-    lon = center.shape[1]
-    west = pltpu.roll(center, 1, 1)
-    west2 = pltpu.roll(center, 2, 1)
-    east = pltpu.roll(center, lon - 1, 1)
-    return (
-        center * (1.0 - step_size - 2.0 * coupling)
-        + step_size * ((east - west2) * west + force)
-        + coupling * (before + after)
-    )
-
-
-def put_line(out_ref, odd, leader, line, value):
-    width = out_ref.shape[2]
-    parts = value.shape[1] // width
-    row = line + odd * (2 * STEPS - 1 - 2 * line)
-    for part in range(parts):
-        chunk = rank_of(row * parts + part, leader, out_ref.shape[0])
-        out_ref[chunk] = value[:, part * width : (part + 1) * width]
-
-
-def near_kernel(after_ref, own_cross_ref, own_near_ref, got_near_ref, done_ref, edge_ref, *levels):
     def start(read):
-        def of(line):
-            if line < STEPS:
-                return read(own_cross_ref, line)
-            if line < 2 * STEPS:
-                return read(own_near_ref, line - STEPS)
-            return read(got_near_ref, 3 * STEPS - 1 - line)
-
-        return of
+        return lambda line: read(own_cross_ref, line) if line < STEPS else read(own_near_ref, 2 * STEPS - 1 - line)
 
     force = start(force_of)
     read = start(state_of)
-    for step in range(1, STEPS + 1):
-        for line in range(step, 3 * STEPS - step):
+    for step in range(1, STEPS):
+        last = 2 * STEPS - 1 - step
+        for line in range(step, last + 1):
             new = advance(read(line - 1), read(line), read(line + 1), force(line))
-            if step == STEPS:
-                done_ref[line - STEPS] = new
-            else:
-                levels[step - 1][line - step] = new
-                if line < step + 2:
-                    edge_ref[2 * (step - 1) + line - step] = new
-        if step < STEPS:
-            read = lambda line, step=step: levels[step - 1][line - step]
-
-
-def cross_kernel(last, strip_ref, done_ref, own_cross_ref, got_cross_ref, edge_ref, out_ref, *levels):
-    strip = strip_ref[0]
-    odd = lax.rem(strip, 2)
-    leader = leader_of(strip)
-    kept = jnp.where(jnp.logical_or(strip == 0, strip == last), 0.0, 1.0)
-
+            levels[step - 1][line - step] = new
+            for edge_ref, at in ((cross_edge_ref, line - step), (near_edge_ref, last - line)):
+                if at < 2:
+                    edge_ref[2 * (step - 1) + at] = new
+        read = lambda line, step=step: levels[step - 1][line - step]
+
+
+def border_lines(own_ref, got_ref, edge_ref, levels, kept, put):
     def start(read):
-        return lambda line: read(own_cross_ref, line) if line >= 0 else read(got_cross_ref, -1 - line)
-
-    for line in range(STEPS):
-        put_line(out_ref, odd, leader, STEPS + line, done_ref[line])
+        return lambda at: read(own_ref, at) if at >= 0 else read(got_ref, -1 - at)
+
     force = start(force_of)
     read = start(state_of)
     for step in range(1, STEPS + 1):
         first = step - STEPS
-        for line in range(first, first + STEPS):
-            new = advance(read(line - 1), read(line), read(line + 1), force(line))
-            if line < 0:
+        for at in range(first, first + STEPS):
+            new = advance(read(at - 1), read(at), read(at + 1), force(at))
+            if at < 0 and kept is not None:
                 new = new * kept
             if step == STEPS:
-                put_line(out_ref, odd, leader, line, new)
+                put(at, new)
             else:
-                levels[step - 1][line - first] = new
+                levels[step - 1][at - first] = new
         if step < STEPS:
 
-            def read(line, step=step, first=first):
-                if line < step:
-                    return levels[step - 1][line - first]
-                return edge_ref[2 * (step - 1) + line - step]
+            def read(at, step=step, first=first):
+                if at < step:
+                    return levels[step - 1][at - first]
+                return edge_ref[2 * (step - 1) + at - step]
+
+
+def near_kernel(own_ref, got_ref, edge_ref, done_ref, *levels):
+    def put(at, value):
+        done_ref[at] = value
+
+    border_lines(own_ref, got_ref, edge_ref, levels, None, put)
+
+
+def cross_kernel(last, strip_ref, columns_ref, done_ref, own_ref, got_ref, edge_ref, out_ref, *levels):
+    strip = strip_ref[0]
+    odd = lax.rem(strip, 2)
+    leader = leader_of(strip)
+    for at in range(STEPS):
+        put_line(out_ref, odd, leader, 2 * STEPS - 1 - at, done_ref[at])
+    kept = jnp.where(jnp.logical_or(strip == 0, strip == last), 0.0, 1.0)
+    put = lambda at, value: put_line(out_ref, odd, leader, at, value)
+    border_lines(own_ref, got_ref, edge_ref, levels, kept, put)
 
 
 NN = (((1,), (0,)), ((), ()))
@@ -311,41 +315,45 @@
     swap = [(i, i ^ 1) for i in range(strips)]
     got_cross = lax.ppermute(cross, "strip", span)
     got_near = lax.ppermute(near, "strip", swap)
-    columns = pl.pallas_call(
-        columns_kernel,
-        out_shape=jax.ShapeDtypeStruct((slots, 4 * regions), jnp.float32),
-        in_specs=[SMEM] + [VMEM] * 3 + [ANY],
-        out_specs=VMEM,
-        compiler_params=params(),
-        cost_estimate=pl.CostEstimate(flops=10**7, bytes_accessed=4096, transcendentals=0),
-        name="columns",
-    )(obs_count, obs_index, obs_value, obs_precision, near)
+
+    def line_slabs(count):
+        return pltpu.VMEM((count, per, lon), jnp.float32)
+
+    edges = jax.ShapeDtypeStruct((2 * (STEPS - 1), per, lon), jnp.float32)
+    border_levels = [line_slabs(STEPS) for _ in range(1, STEPS)]
+    columns, cross_edge, near_edge = pl.pallas_call(
+        own_kernel,
+        out_shape=(jax.ShapeDtypeStruct((slots, 4 * regions), jnp.float32), edges, edges),
+        in_specs=[SMEM] + [VMEM] * 5,
+        out_specs=(VMEM,) * 3,
+        scratch_shapes=[line_slabs(2 * STEPS - 2 * step) for step in range(1, STEPS)],
+        compiler_params=params(),
+        cost_estimate=pl.CostEstimate(flops=10**8, bytes_accessed=4096, transcendentals=0),
+        name="forecast_own",
+    )(obs_count, obs_index, obs_value, obs_precision, cross, near)
     chunks = lax.axis_size("mem")
     width = rows * lon // chunks
     full = jax.ShapeDtypeStruct((chunks, per, width), jnp.float32)
 
-    def line_slabs(count):
-        return pltpu.VMEM((count, per, lon), jnp.float32)
-
-    done, edges = pl.pallas_call(
+    done = pl.pallas_call(
         near_kernel,
-        out_shape=tuple(jax.ShapeDtypeStruct((count, per, lon), jnp.float32) for count in (STEPS, 2 * (STEPS - 1))),
-        in_specs=[ANY] + [VMEM] * 3,
-        out_specs=(VMEM, VMEM),
-        scratch_shapes=[line_slabs(3 * STEPS - 2 * step) for step in range(1, STEPS)],
+        out_shape=jax.ShapeDtypeStruct((STEPS, per, lon), jnp.float32),
+        in_specs=[VMEM] * 3,
+        out_specs=VMEM,
+        scratch_shapes=border_levels,
         compiler_params=params(),
         cost_estimate=pl.CostEstimate(flops=10**8, bytes_accessed=4096, transcendentals=0),
         name="forecast_near",
-    )(columns, cross, near, got_near)
+    )(near, got_near, near_edge)
     sent = pl.pallas_call(
         functools.partial(cross_kernel, strips - 1),
         out_shape=full,
-        in_specs=[SMEM] + [VMEM] * 4,
+        in_specs=[SMEM, ANY] + [VMEM] * 4,
         out_specs=VMEM,
-        scratch_shapes=[line_slabs(STEPS) for _ in range(1, STEPS)],
+        scratch_shapes=border_levels,
         compiler_params=params(),
         name="forecast_cross",
-    )(strip, done, cross, got_cross, edges)
+    )(strip, columns, done, cross, got_cross, cross_edge)
     groups = [
         [i * chunks + (leader_of(i) + rank) % chunks for rank in range(chunks)] for i in range(strips)
     ]

time: 72.1 us -> 71.5 us (level)
  no operation moved by 1% of the time
where the time goes in v6:
time: 71.5 us; the launch traced here: 71.2 us
  blocking collectives  52.7 us (74%)
  Pallas kernels  6.95 us (10%)
  starting transfers between devices  5.94 us (8%)
  waiting for transfers between devices  3.6 us (5%)
  local copies, waits for them, and re-layouts  1.91 us (3%)
    all_to_all x2, blocking collectives, exchange(): lax.all_to_all(x, ('strip', 'mem'), split_axis=0, concat_axis=0, axis_ind...  52.7 us
    ppermute x1, waiting for transfers between devices, local(): got_cross = lax.ppermute(cross, 'strip', span)  3.6 us
    ppermute x1, starting transfers between devices, local(): got_cross = lax.ppermute(cross, 'strip', span)  3.22 us
    ppermute x1, starting transfers between devices, local(): got_near = lax.ppermute(near, 'strip', swap)  2.72 us
    pallas_call x1, Pallas kernels, local(): pl.pallas_call(analysis_kernel, out_shape=jax.ShapeDtypeStruct((chunks, p...  2.66 us
    unnamed x12, local copies, waits for them, and re-layouts  1.91 us
  transfers between devices with their start and end apart: 2, of which 1 were waited for; matrix products, arithmetic and copies ran while one was open for 0% of the time, Pallas kernels for 3%

profile of v6, /device:TPU:3, one launch (start us, length us, event | category | flops | bytes accessed | tf_op | source)
XLA Modules:
  0.0 71.2 jit_solution(16068012975452583471)
XLA Ops:
  0.0 0.0 copy-start
  0.0 1.0 %copy-done = f32[8,8,2048]{2,1,0:T(8,128)S(1)} copy-done((f32[8,8,2048]{2,1,0:T(8,128)S(1)}, f32[8,8,2048]{2,1,0:T(8,128)}, u32[]{:S(2)}) %copy-start) | copy-done | bytes 524312
  1.0 0.0 copy-start.1
  1.0 0.8 %copy-done.1 = f32[8,2048]{1,0:T(8,128)S(1)} copy-done((f32[8,2048]{1,0:T(8,128)S(1)}, f32[8,2048]{1,0:T(8,128)}, u32[]{:S(2)}) %copy-start.1) | copy-done | bytes 65560
  1.9 0.1 pack.1
  2.0 0.0 copy-start.3
  2.0 0.0 copy-start.4
  2.0 0.0 copy-start.2
  2.1 0.0 copy-start.5
  2.1 2.7 %collective-permute-start = (f32[9,8,1024]{2,1,0:T(8,128)S(1)}, f32[9,8,1024]{2,1,0:T(8,128)S(1)}, u32[]{:S(2)}, u32[]{:S(2)}) collective-permute-start(f32[9,8,1024]{2,1,0:T(8,128)S(1)} %get-tuple-element.11.own_near_ref.own_ref), channel_id=1, source_target_pairs={{0,1},{1,0},{2,3},{3,2},{4,5},{5,4},{6,7},{7,6},{8,9},{9,8},{10,11... | collective-permute-start | bytes 884744 | tf_op jit(solution)/shard_map/ppermute | solution.py:317
  4.8 3.2 %collective-permute-start.1 = (f32[9,8,1024]{2,1,0:T(8,128)S(1)}, f32[9,8,1024]{2,1,0:T(8,128)S(1)}, u32[]{:S(2)}, u32[]{:S(2)}) collective-permute-start(f32[9,8,1024]{2,1,0:T(8,128)S(1)} %get-tuple-element.10.own_cross_ref.own_ref), channel_id=1, source_target_pairs={{1,2},{3,4},{5,6},{7,8},{9,10},{11,12},{13,14},{15,16},{17,18},{19... | collective-permute-start | bytes 884744 | tf_op jit(solution)/shard_map/ppermute | solution.py:316
  8.0 0.0 copy-done.3
  8.0 0.0 copy-done.4
  8.0 0.0 copy-done.2
  8.0 0.0 copy-done.5
  8.1 1.3 %forecast_own.1 = (f32[128,8]{1,0:T(8,128)S(1)}, f32[6,8,2048]{2,1,0:T(8,128)S(1)}, f32[6,8,2048]{2,1,0:T(8,128)S(1)}) custom-call(s32[2]{0:T(128)S(1)} %copy-done.5, s32[2,128]{1,0:T(2,128)S(1)} %copy-done.2, f32[2,128]{1,0:T(2,128)S(1)} %copy-done.3, f32[2,128]{1,0:T(2,128)S(1)} %copy-done.4, f32[9,8,1024]{2,1,0:T(8,128)S(1)} %get-tuple-element.10.own_cross_ref.own_ref, ...), custom_call_target="tpu_custom_call" | custom-call | flops 100000000 | bytes 4096 | tf_op jit(solution)/shard_map/forecast_own/pallas_call | solution.py:324
  9.4 0.0 collective-permute-done.got_ref
  9.4 0.9 %forecast_near.1.done_ref = f32[4,8,2048]{2,1,0:T(8,128)S(1)} custom-call(f32[9,8,1024]{2,1,0:T(8,128)S(1)} %get-tuple-element.11.own_near_ref.own_ref, f32[9,8,1024]{2,1,0:T(8,128)S(1)} %collective-permute-done.got_ref, f32[6,8,2048]{2,1,0:T(8,128)S(1)} %get-tuple-element.13.edge_ref), custom_call_target="tpu_custom_call" | custom-call | flops 100000000 | bytes 4096 | tf_op jit(solution)/shard_map/forecast_near/pallas_call | solution.py:338
  10.4 3.6 %collective-permute-done.1.got_ref = f32[9,8,1024]{2,1,0:T(8,128)S(1)} collective-permute-done((f32[9,8,1024]{2,1,0:T(8,128)S(1)}, f32[9,8,1024]{2,1,0:T(8,128)S(1)}, u32[]{:S(2)}, u32[]{:S(2)}) %collective-permute-start.1) | collective-permute-done | bytes 294944 | tf_op jit(solution)/shard_map/ppermute | solution.py:316
  13.9 0.9 %forecast_cross.1 = f32[32,8,512]{2,1,0:T(8,128)S(1)} custom-call(s32[1]{0:T(128)} %bitcast.strip_ref, f32[128,8]{1,0:T(8,128)S(1)} %get-tuple-element.12.columns_ref, f32[4,8,2048]{2,1,0:T(8,128)S(1)} %forecast_near.1.done_ref, f32[9,8,1024]{2,1,0:T(8,128)S(1)} %get-tuple-element.10.own_cross_ref.own_ref, f32[9,8,1024]{2,1,0:T(8,128)S(1)} %collective-permute-done.1.got_ref, ...), custom_call_target="tpu_custom_call" | custom-call | tf_op jit(solution)/shard_map/forecast_cross/pallas_call | solution.py:348
  14.9 31.1 %all_to_all.10.block_ref = f32[32,8,512]{2,1,0:T(8,128)S(1)} all-to-all(f32[32,8,512]{2,1,0:T(8,128)S(1)} %forecast_cross.1), channel_id=1, replica_groups={{0,32,64,96,128,160,192,224,256,288,320,352,384,416,448,480,512,544,576..., dimensions={0} | all-to-all | bytes 1048576 | tf_op jit(solution)/shard_map/all_to_all | solution.py:362
  46.0 2.7 %analysis.1 = f32[32,8,512]{2,1,0:T(8,128)S(1)} custom-call(f32[128,8]{1,0:T(8,128)S(1)} %get-tuple-element.12.columns_ref, f32[32,8,512]{2,1,0:T(8,128)S(1)} %all_to_all.10.block_ref), custom_call_target="tpu_custom_call" | custom-call | tf_op jit(solution)/shard_map/analysis/pallas_call | solution.py:365
  48.6 21.6 %all_to_all.11.block_ref = f32[32,8,512]{2,1,0:T(8,128)S(1)} all-to-all(f32[32,8,512]{2,1,0:T(8,128)S(1)} %analysis.1), channel_id=1, replica_groups={{0,32,64,96,128,160,192,224,256,288,320,352,384,416,448,480,512,544,576..., dimensions={0} | all-to-all | bytes 1048576 | tf_op jit(solution)/shard_map/all_to_all | solution.py:362
  70.2 0.9 %unpack.1 = f32[8,8,2048]{2,1,0:T(8,128)} custom-call(s32[1]{0:T(128)} %bitcast.strip_ref, f32[32,8,512]{2,1,0:T(8,128)S(1)} %all_to_all.11.block_ref), custom_call_target="tpu_custom_call" | custom-call | tf_op jit(solution)/shard_map/unpack/pallas_call | solution.py:374
Async XLA Ops:
  0.0 1.0 %copy-start = (f32[8,8,2048]{2,1,0:T(8,128)S(1)}, f32[8,8,2048]{2,1,0:T(8,128)}, u32[]{:S(2)}) copy-start(f32[8,8,2048]{2,1,0:T(8,128)} %ens_ref.1) | copy-start | bytes 1572868
  1.0 0.8 %copy-start.1 = (f32[8,2048]{1,0:T(8,128)S(1)}, f32[8,2048]{1,0:T(8,128)}, u32[]{:S(2)}) copy-start(f32[8,2048]{1,0:T(8,128)} %forcing_ref.1) | copy-start | bytes 196612
  2.0 6.0 %copy-start.3 = (f32[2,128]{1,0:T(2,128)S(1)}, f32[2,128]{1,0:T(2,128)}, u32[]{:S(2)}) copy-start(f32[2,128]{1,0:T(2,128)} %value_ref.1) | copy-start | bytes 3076
  2.0 6.0 %copy-start.4 = (f32[2,128]{1,0:T(2,128)S(1)}, f32[2,128]{1,0:T(2,128)}, u32[]{:S(2)}) copy-start(f32[2,128]{1,0:T(2,128)} %precision_ref.1) | copy-start | bytes 3076
  2.0 6.0 %copy-start.2 = (s32[2,128]{1,0:T(2,128)S(1)}, s32[2,128]{1,0:T(2,128)}, u32[]{:S(2)}) copy-start(s32[2,128]{1,0:T(2,128)} %index_ref.1) | copy-start | bytes 3076
  2.1 6.0 %copy-start.5 = (s32[2]{0:T(128)S(1)}, s32[2]{0:T(128)}, u32[]{:S(2)}) copy-start(s32[2]{0:T(128)} %count_ref.1) | copy-start | bytes 28
  2.1 7.3 %collective-permute-start = (f32[9,8,1024]{2,1,0:T(8,128)S(1)}, f32[9,8,1024]{2,1,0:T(8,128)S(1)}, u32[]{:S(2)}, u32[]{:S(2)}) collective-permute-start(f32[9,8,1024]{2,1,0:T(8,128)S(1)} %get-tuple-element.11.own_near_ref.own_ref), channel_id=1, source_target_pairs={{0,1},{1,0},{2,3},{3,2},{4,5},{5,4},{6,7},{7,6},{8,9},{9,8},{10,11... | collective-permute-start | bytes 884744 | tf_op jit(solution)/shard_map/ppermute | solution.py:317
  4.8 9.2 %collective-permute-start.1 = (f32[9,8,1024]{2,1,0:T(8,128)S(1)}, f32[9,8,1024]{2,1,0:T(8,128)S(1)}, u32[]{:S(2)}, u32[]{:S(2)}) collective-permute-start(f32[9,8,1024]{2,1,0:T(8,128)S(1)} %get-tuple-element.10.own_cross_ref.own_ref), channel_id=1, source_target_pairs={{1,2},{3,4},{5,6},{7,8},{9,10},{11,12},{13,14},{15,16},{17,18},{19... | collective-permute-start | bytes 884744 | tf_op jit(solution)/shard_map/ppermute | solution.py:316

commit v7 on v6

--- a/solution.py
+++ b/solution.py
@@ -38,30 +38,41 @@
     return line if parity == 0 else 2 * STEPS - 1 - line
 
 
-def pack_kernel(strip_ref, ens_ref, forcing_ref, cross_ref, near_ref):
+def pack_kernel(strip_ref, ens_ref, forcing_ref, cross_ref, near_ref, held_ref, force_ref, arrived):
     odd = lax.rem(strip_ref[0], 2)
     half = cross_ref.shape[2]
-    for parity in (0, 1):
-
-        @pl.when(odd == parity)
-        def _():
-            for line in range(2 * STEPS):
-                inner = line < STEPS
-                message, at = (cross_ref, line) if inner else (near_ref, 2 * STEPS - 1 - line)
-                row = row_of(line, parity)
-                state, force = ens_ref[:, row, :], forcing_ref[row : row + 1, :]
-                for side in range(2):
-                    lons = slice(side * half, (side + 1) * half)
-                    message[2 * at + side] = state[:, lons]
-                    spot = side * STEPS + at
-                    message[2 * STEPS, spot : spot + 1, :] = force[:, lons]
+    lons = [pl.ds(side * half, half) for side in range(2)]
+    copies = [pltpu.make_async_copy(forcing_ref, force_ref, arrived.at[2])]
+    copies += [
+        pltpu.make_async_copy(ens_ref.at[:, :, lons[side]], held_ref.at[side], arrived.at[side])
+        for side in range(2)
+    ]
+    for copy in copies:
+        copy.start()
+    copies[0].wait()
+    for side in range(2):
+        copies[1 + side].wait()
+        for parity in (0, 1):
+
+            @pl.when(odd == parity)
+            def _():
+                for line in range(2 * STEPS):
+                    inner = line < STEPS
+                    message, at = (cross_ref, line) if inner else (near_ref, 2 * STEPS - 1 - line)
+                    row, spot = row_of(line, parity), side * STEPS + at
+                    message[2 * at + side] = held_ref[side, :, row, :]
+                    message[2 * STEPS, spot : spot + 1, :] = force_ref[row : row + 1, lons[side]]
 
 
 def state_of(message, at):
+    if isinstance(message, tuple):
+        return state_of(message[0], at) + state_of(message[1], at)
     return jnp.concatenate([message[2 * at], message[2 * at + 1]], axis=1)
 
 
 def force_of(message, at):
+    if isinstance(message, tuple):
+        return force_of(message[0], at) + force_of(message[1], at)
     both = [message[2 * STEPS, spot : spot + 1, :] for spot in (at, STEPS + at)]
     return jnp.concatenate(both, axis=1)
 
@@ -152,7 +163,7 @@
     border_lines(own_ref, got_ref, edge_ref, levels, None, put)
 
 
-def cross_kernel(last, strip_ref, columns_ref, done_ref, own_ref, got_ref, edge_ref, out_ref, *levels):
+def cross_kernel(last, strip_ref, columns_ref, done_ref, own_ref, got_early_ref, got_late_ref, edge_ref, out_ref, *levels):
     strip = strip_ref[0]
     odd = lax.rem(strip, 2)
     leader = leader_of(strip)
@@ -160,7 +171,7 @@
         put_line(out_ref, odd, leader, 2 * STEPS - 1 - at, done_ref[at])
     kept = jnp.where(jnp.logical_or(strip == 0, strip == last), 0.0, 1.0)
     put = lambda at, value: put_line(out_ref, odd, leader, at, value)
-    border_lines(own_ref, got_ref, edge_ref, levels, kept, put)
+    border_lines(own_ref, (got_early_ref, got_late_ref), edge_ref, levels, kept, put)
 
 
 NN = (((1,), (0,)), ((), ()))
@@ -305,16 +316,24 @@
     cross, near = pl.pallas_call(
         pack_kernel,
         out_shape=(message, message),
-        in_specs=[SMEM, VMEM, VMEM],
+        in_specs=[SMEM, ANY, ANY],
         out_specs=(VMEM, VMEM),
+        scratch_shapes=[
+            pltpu.VMEM((2, per, rows, lon // 2), jnp.float32),
+            pltpu.VMEM((rows, lon), jnp.float32),
+            pltpu.SemaphoreType.DMA((3,)),
+        ],
         compiler_params=params(),
         name="pack",
-    )(strip, ensemble, forcing)
-    span = [(i, i + 1) for i in range(1, strips - 1, 2)]
-    span = span + [(b, a) for a, b in span]
-    swap = [(i, i ^ 1) for i in range(strips)]
-    got_cross = lax.ppermute(cross, "strip", span)
-    got_near = lax.ppermute(near, "strip", swap)
+    )(strip, *(pltpu.with_memory_space_constraint(x, pltpu.HBM) for x in (ensemble, forcing)))
+
+    def swap(message, lows):
+        pairs = [(i, i + 1) for i in lows]
+        return lax.ppermute(message, "strip", pairs + [(b, a) for a, b in pairs])
+
+    got_early = swap(cross, range(1, strips - 1, 4))
+    got_near = swap(near, range(0, strips, 2))
+    got_late = swap(cross, range(3, strips - 1, 4))
 
     def line_slabs(count):
         return pltpu.VMEM((count, per, lon), jnp.float32)
@@ -348,12 +367,12 @@
     sent = pl.pallas_call(
         functools.partial(cross_kernel, strips - 1),
         out_shape=full,
-        in_specs=[SMEM, ANY] + [VMEM] * 4,
+        in_specs=[SMEM, ANY] + [VMEM] * 5,
         out_specs=VMEM,
         scratch_shapes=border_levels,
         compiler_params=params(),
         name="forecast_cross",
-    )(strip, columns, done, cross, got_cross, cross_edge)
+    )(strip, columns, done, cross, got_early, got_late, cross_edge)
     groups = [
         [i * chunks + (leader_of(i) + rank) % chunks for rank in range(chunks)] for i in range(strips)
     ]

time: 71.5 us -> 71.9 us (level)
  blocking collectives: 52.7 us -> 54.6 us
  local copies, waits for them, and re-layouts: 1.91 us -> 0.03 us
  waiting for transfers between devices: 3.6 us -> 2.23 us
  Pallas kernels: 6.95 us -> 7.99 us
    all_to_all x2, blocking collectives: 52.7 us -> 54.6 us  [exchange(): lax.all_to_all(x, ('strip', 'mem'), split_axis=0, concat_axis=0, axis_ind...]
    unnamed x12 -> x8, local copies, waits for them, and re-layouts: 1.91 us -> 0.03 us
    ppermute x2 -> x3, waiting for transfers between devices: 3.6 us -> 2.23 us  [swap(): return lax.ppermute(message, 'strip', pairs + [(b, a) for a, b in pairs])]
    pallas_call x1, Pallas kernels: 0.13 us -> 1.15 us  [local(): pl.pallas_call(pack_kernel, out_shape=(message, message), in_specs=[SMEM,...]
    ppermute x2 -> x3, starting transfers between devices: 5.94 us -> 6.61 us  [swap(): return lax.ppermute(message, 'strip', pairs + [(b, a) for a, b in pairs])]
  transfers between devices with their start and end apart: 2 -> 3, of which waited for: 1 -> 1; matrix products, arithmetic and copies ran while one was open for 0% -> 0% of each run, Pallas kernels for 3% -> 3%
where the time goes in v7:
time: 71.9 us; the launch traced here: 71.6 us
  blocking collectives  54.6 us (76%)
  Pallas kernels  7.99 us (11%)
  starting transfers between devices  6.61 us (9%)
  waiting for transfers between devices  2.23 us (3%)
    all_to_all x2, blocking collectives, exchange(): lax.all_to_all(x, ('strip', 'mem'), split_axis=0, concat_axis=0, axis_ind...  54.6 us
    ppermute x3, starting transfers between devices, swap(): return lax.ppermute(message, 'strip', pairs + [(b, a) for a, b in pairs])  6.61 us
    pallas_call x1, Pallas kernels, local(): pl.pallas_call(analysis_kernel, out_shape=jax.ShapeDtypeStruct((chunks, p...  2.65 us
    ppermute x3, waiting for transfers between devices, swap(): return lax.ppermute(message, 'strip', pairs + [(b, a) for a, b in pairs])  2.23 us
  transfers between devices with their start and end apart: 3, of which 1 were waited for; matrix products, arithmetic and copies ran while one was open for 0% of the time, Pallas kernels for 3%

profile of v7, /device:TPU:3, one launch (start us, length us, event | category | flops | bytes accessed | tf_op | source)
XLA Modules:
  0.0 71.6 jit_solution(13125712573262703274)
XLA Ops:
  0.0 1.2 %pack.1 = (f32[9,8,1024]{2,1,0:T(8,128)S(1)}, f32[9,8,1024]{2,1,0:T(8,128)S(1)}) custom-call(s32[1]{0:T(128)} %bitcast.strip_ref, f32[8,8,2048]{2,1,0:T(8,128)} %ens_ref.1, f32[8,2048]{1,0:T(8,128)} %forcing_ref.1), custom_call_target="tpu_custom_call" | custom-call | tf_op jit(solution)/shard_map/pack/pallas_call | solution.py:316
  1.2 0.0 copy-start.1
  1.2 0.0 copy-start.2
  1.2 0.0 copy-start
  1.2 0.0 copy-start.3
  1.2 2.7 %collective-permute-start = (f32[9,8,1024]{2,1,0:T(8,128)S(1)}, f32[9,8,1024]{2,1,0:T(8,128)S(1)}, u32[]{:S(2)}, u32[]{:S(2)}) collective-permute-start(f32[9,8,1024]{2,1,0:T(8,128)S(1)} %get-tuple-element.11.own_near_ref.own_ref), channel_id=1, source_target_pairs={{0,1},{2,3},{4,5},{6,7},{8,9},{10,11},{12,13},{14,15},{16,17},{18,... | collective-permute-start | bytes 884744 | tf_op jit(solution)/shard_map/ppermute | solution.py:332
  3.9 3.2 %collective-permute-start.1 = (f32[9,8,1024]{2,1,0:T(8,128)S(1)}, f32[9,8,1024]{2,1,0:T(8,128)S(1)}, u32[]{:S(2)}, u32[]{:S(2)}) collective-permute-start(f32[9,8,1024]{2,1,0:T(8,128)S(1)} %get-tuple-element.10.own_cross_ref.own_ref), channel_id=1, source_target_pairs={{1,2},{5,6},{9,10},{13,14},{17,18},{21,22},{25,26},{29,30},{2,1},{... | collective-permute-start | bytes 884744 | tf_op jit(solution)/shard_map/ppermute | solution.py:332
  7.2 0.7 collective-permute-start.2
  7.8 0.0 copy-done.1
  7.9 0.0 copy-done.2
  7.9 0.0 copy-done
  7.9 0.0 copy-done.3
  7.9 1.3 %forecast_own.1 = (f32[128,8]{1,0:T(8,128)S(1)}, f32[6,8,2048]{2,1,0:T(8,128)S(1)}, f32[6,8,2048]{2,1,0:T(8,128)S(1)}) custom-call(s32[2]{0:T(128)S(1)} %copy-done.3, s32[2,128]{1,0:T(2,128)S(1)} %copy-done, f32[2,128]{1,0:T(2,128)S(1)} %copy-done.1, f32[2,128]{1,0:T(2,128)S(1)} %copy-done.2, f32[9,8,1024]{2,1,0:T(8,128)S(1)} %get-tuple-element.10.own_cross_ref.own_ref, ...), custom_call_target="tpu_custom_call" | custom-call | flops 100000000 | bytes 4096 | tf_op jit(solution)/shard_map/forecast_own/pallas_call | solution.py:343
  9.2 0.0 collective-permute-done.got_ref
  9.2 0.9 %forecast_near.1.done_ref = f32[4,8,2048]{2,1,0:T(8,128)S(1)} custom-call(f32[9,8,1024]{2,1,0:T(8,128)S(1)} %get-tuple-element.11.own_near_ref.own_ref, f32[9,8,1024]{2,1,0:T(8,128)S(1)} %collective-permute-done.got_ref, f32[6,8,2048]{2,1,0:T(8,128)S(1)} %get-tuple-element.13.edge_ref), custom_call_target="tpu_custom_call" | custom-call | flops 100000000 | bytes 4096 | tf_op jit(solution)/shard_map/forecast_near/pallas_call | solution.py:357
  10.2 2.2 %collective-permute-done.1.got_early_ref = f32[9,8,1024]{2,1,0:T(8,128)S(1)} collective-permute-done((f32[9,8,1024]{2,1,0:T(8,128)S(1)}, f32[9,8,1024]{2,1,0:T(8,128)S(1)}, u32[]{:S(2)}, u32[]{:S(2)}) %collective-permute-start.1) | collective-permute-done | bytes 294944 | tf_op jit(solution)/shard_map/ppermute | solution.py:332
  12.4 0.0 collective-permute-done.2.got_late_ref
  12.4 1.0 %forecast_cross.1 = f32[32,8,512]{2,1,0:T(8,128)S(1)} custom-call(s32[1]{0:T(128)} %bitcast.strip_ref, f32[128,8]{1,0:T(8,128)S(1)} %get-tuple-element.12.columns_ref, f32[4,8,2048]{2,1,0:T(8,128)S(1)} %forecast_near.1.done_ref, f32[9,8,1024]{2,1,0:T(8,128)S(1)} %get-tuple-element.10.own_cross_ref.own_ref, ...), custom_call_target="tpu_custom_call" | custom-call | tf_op jit(solution)/shard_map/forecast_cross/pallas_call | solution.py:367
  13.4 32.0 %all_to_all.10.block_ref = f32[32,8,512]{2,1,0:T(8,128)S(1)} all-to-all(f32[32,8,512]{2,1,0:T(8,128)S(1)} %forecast_cross.1), channel_id=1, replica_groups={{0,32,64,96,128,160,192,224,256,288,320,352,384,416,448,480,512,544,576..., dimensions={0} | all-to-all | bytes 1048576 | tf_op jit(solution)/shard_map/all_to_all | solution.py:381
  45.4 2.6 %analysis.1 = f32[32,8,512]{2,1,0:T(8,128)S(1)} custom-call(f32[128,8]{1,0:T(8,128)S(1)} %get-tuple-element.12.columns_ref, f32[32,8,512]{2,1,0:T(8,128)S(1)} %all_to_all.10.block_ref), custom_call_target="tpu_custom_call" | custom-call | tf_op jit(solution)/shard_map/analysis/pallas_call | solution.py:384
  48.1 22.6 %all_to_all.11.block_ref = f32[32,8,512]{2,1,0:T(8,128)S(1)} all-to-all(f32[32,8,512]{2,1,0:T(8,128)S(1)} %analysis.1), channel_id=1, replica_groups={{0,32,64,96,128,160,192,224,256,288,320,352,384,416,448,480,512,544,576..., dimensions={0} | all-to-all | bytes 1048576 | tf_op jit(solution)/shard_map/all_to_all | solution.py:381
  70.7 0.9 %unpack.1 = f32[8,8,2048]{2,1,0:T(8,128)} custom-call(s32[1]{0:T(128)} %bitcast.strip_ref, f32[32,8,512]{2,1,0:T(8,128)S(1)} %all_to_all.11.block_ref), custom_call_target="tpu_custom_call" | custom-call | tf_op jit(solution)/shard_map/unpack/pallas_call | solution.py:393
Async XLA Ops:
  1.2 6.7 %copy-start.1 = (f32[2,128]{1,0:T(2,128)S(1)}, f32[2,128]{1,0:T(2,128)}, u32[]{:S(2)}) copy-start(f32[2,128]{1,0:T(2,128)} %value_ref.1) | copy-start | bytes 3076
  1.2 6.7 %copy-start.2 = (f32[2,128]{1,0:T(2,128)S(1)}, f32[2,128]{1,0:T(2,128)}, u32[]{:S(2)}) copy-start(f32[2,128]{1,0:T(2,128)} %precision_ref.1) | copy-start | bytes 3076
  1.2 6.7 %copy-start = (s32[2,128]{1,0:T(2,128)S(1)}, s32[2,128]{1,0:T(2,128)}, u32[]{:S(2)}) copy-start(s32[2,128]{1,0:T(2,128)} %index_ref.1) | copy-start | bytes 3076
  1.2 6.7 %copy-start.3 = (s32[2]{0:T(128)S(1)}, s32[2]{0:T(128)}, u32[]{:S(2)}) copy-start(s32[2]{0:T(128)} %count_ref.1) | copy-start | bytes 28
  1.2 8.0 %collective-permute-start = (f32[9,8,1024]{2,1,0:T(8,128)S(1)}, f32[9,8,1024]{2,1,0:T(8,128)S(1)}, u32[]{:S(2)}, u32[]{:S(2)}) collective-permute-start(f32[9,8,1024]{2,1,0:T(8,128)S(1)} %get-tuple-element.11.own_near_ref.own_ref), channel_id=1, source_target_pairs={{0,1},{2,3},{4,5},{6,7},{8,9},{10,11},{12,13},{14,15},{16,17},{18,... | collective-permute-start | bytes 884744 | tf_op jit(solution)/shard_map/ppermute | solution.py:332
  3.9 8.5 %collective-permute-start.1 = (f32[9,8,1024]{2,1,0:T(8,128)S(1)}, f32[9,8,1024]{2,1,0:T(8,128)S(1)}, u32[]{:S(2)}, u32[]{:S(2)}) collective-permute-start(f32[9,8,1024]{2,1,0:T(8,128)S(1)} %get-tuple-element.10.own_cross_ref.own_ref), channel_id=1, source_target_pairs={{1,2},{5,6},{9,10},{13,14},{17,18},{21,22},{25,26},{29,30},{2,1},{... | collective-permute-start | bytes 884744 | tf_op jit(solution)/shard_map/ppermute | solution.py:332
  7.2 5.2 %collective-permute-start.2 = (f32[9,8,1024]{2,1,0:T(8,128)S(1)}, f32[9,8,1024]{2,1,0:T(8,128)S(1)}, u32[]{:S(2)}, u32[]{:S(2)}) collective-permute-start(f32[9,8,1024]{2,1,0:T(8,128)S(1)} %get-tuple-element.10.own_cross_ref.own_ref), channel_id=1, source_target_pairs={{3,4},{7,8},{11,12},{15,16},{19,20},{23,24},{27,28},{4,3},{8,7},{1... | collective-permute-start | bytes 884744 | tf_op jit(solution)/shard_map/ppermute | solution.py:332
